TPU v7x, 32 devices: a whole 2x2x4 slice. The times are simulated.
32 devices in a mesh: row: 8 (over y, x, core), col: 4 (over z).
Axes of the slice: x: 2, y: 2, z: 4, core: 2. Of those that a mesh axis runs over, the one named last changes fastest.
Arguments:
- features: bfloat16 [65536, 256], P(('row', 'col')), may hold values from -6 to 6
- tiles: bfloat16 [8, 4, 768, 128, 128], P('row', 'col'), as said below
- tile_rows: int32 [8, 4, 768], P('row', 'col'), may hold values from 0 to 63
- tile_cols: int32 [8, 4, 768], P('row', 'col'), may hold values from 0 to 127
- valid: int32 [8, 4, 768], P('row', 'col'), may hold values from 0 to 1, as said below
- weight: bfloat16 [256, 256], replicated, may hold values from -0.375 to 0.375
- bias: float32 [256], replicated, may hold values from -3 to 3
Outputs:
- hidden: bfloat16 [65536, 256], P(('row', 'col'))
Inputs may be any that keep to these rules, and one draw needn't show every extreme that they name: Each cell holds between 96 and 384 valid slots at any positions; in every draw some cell has exactly 384 valid slots. `tiles`: tile entries are non-negative.
All inputs are finite; a program needn't handle non-finite values.
Results may differ from a plain program's by a relative error of at most 0.0039.
Values may be sent and summed in bfloat16 or wider, within the bound.
No kernel may reach another device: no remote copies, remote signals or barrier semaphores. Data moves between devices by JAX's collectives and lax.ppermute only.
A program may use at most 256 MiB of HBM per device.

v0:
```python
import functools

import jax
import jax.numpy as jnp
from jax import lax
from jax.experimental import pallas as pl
from jax.experimental.pallas import tpu as pltpu
from jax.sharding import PartitionSpec as P


LANES = 128
GROUP = 2
UNROLL = 16
STAGES = 4
BATCH = GROUP * UNROLL


def channel_chunks(width):
    lanes = LANES if width % LANES == 0 else width
    return [(start, lanes) for start in range(0, width, lanes)]


def plan_groups(cell_rows, cell_cols, cell_valid, row_tiles, col_bits):
    slots = cell_rows.shape[0]
    live = cell_valid > 0
    row_ids = jnp.arange(row_tiles, dtype=jnp.int32)
    slot_ids = jnp.arange(slots, dtype=jnp.int32)
    hits = (cell_rows[:, None] == row_ids[None, :]) & live[:, None]
    counts = jnp.sum(hits.astype(jnp.int32), axis=0)
    groups = (counts + (GROUP - 1)) // GROUP
    total = jnp.sum(groups)
    before = jnp.sum(jnp.where(row_ids[None, :] < cell_rows[:, None], groups[None, :], 0), axis=1)
    same = (cell_rows[:, None] == cell_rows[None, :]) & live[None, :] & (slot_ids[None, :] < slot_ids[:, None])
    rank = jnp.sum(same.astype(jnp.int32), axis=1)
    place = jnp.where(live, before * GROUP + rank, -1)
    room = -(-(slots + row_tiles * (GROUP - 1)) // BATCH) * BATCH
    seats = jnp.arange(room, dtype=jnp.int32)
    code = slot_ids * (1 << col_bits) + cell_cols + 1
    entries = jnp.sum(jnp.where(seats[:, None] == place[None, :], code[None, :], 0), axis=1) - 1
    ends = jnp.sum(jnp.where(row_ids[:, None] >= row_ids[None, :], groups[None, :], 0), axis=1)
    group_ids = jnp.arange(room // GROUP, dtype=jnp.int32)
    group_rows = jnp.sum((ends[None, :] <= group_ids[:, None]).astype(jnp.int32), axis=1)
    group_rows = jnp.minimum(group_rows, row_tiles - 1)
    turns = (total + (UNROLL - 1)) // UNROLL
    return entries, group_rows, turns.reshape(1)


def tile_kernel(entries, group_rows, turns, place, picks, *refs, parts, col_bits, narrow, wide):
    blocks = refs[:parts]
    tiles = refs[parts]
    outs = refs[parts + 1 : parts + 1 + narrow + wide]
    sums, panel, ring, tile_sems = refs[parts + 1 + narrow + wide :]
    block_tiles = panel.shape[0] // parts
    count = turns[0]
    zero_seat = STAGES * BATCH

    def fetch(turn, seats=range(BATCH)):
        stage = lax.rem(turn, STAGES)
        for seat in seats:
            slot = lax.shift_right_logical(jnp.maximum(entries[turn * BATCH + seat], 0), col_bits)
            pltpu.make_async_copy(tiles.at[slot], ring.at[stage * BATCH + seat], tile_sems.at[stage]).start()

    def arrive(turn):
        stage = lax.rem(turn, STAGES)
        pltpu.make_async_copy(
            tiles.at[pl.ds(0, BATCH)], ring.at[pl.ds(stage * BATCH, BATCH)], tile_sems.at[stage]
        ).wait()

    lax.fori_loop(0, jnp.minimum(count, STAGES - 1), lambda turn, carry: fetch(turn) or carry, 0)
    ring[zero_seat] = jnp.zeros(ring.shape[1:], ring.dtype)
    sums[...] = jnp.zeros(sums.shape, sums.dtype)
    for part in range(parts):
        panel[pl.ds(place[part] * block_tiles, block_tiles)] = blocks[part][...]

    def step(ahead, turn, carry):
        base = lax.rem(turn, STAGES) * BATCH
        arrive(turn)
        products = []
        for group in range(UNROLL):
            if ahead:
                fetch(turn + ahead, range(group * GROUP, (group + 1) * GROUP))
            left, right = [], []
            for member in range(GROUP):
                seat = group * GROUP + member
                entry = entries[turn * BATCH + seat]
                left.append(ring[jnp.where(entry < 0, zero_seat, base + seat)])
                right.append(panel[jnp.maximum(entry, 0) & ((1 << col_bits) - 1)])
            products.append(
                jnp.dot(
                    jnp.concatenate(left, axis=1),
                    jnp.concatenate(right, axis=0),
                    preferred_element_type=jnp.float32,
                )
            )
        for group in range(UNROLL):
            sums[group_rows[turn * UNROLL + group]] += products[group]
        return carry

    steady = jnp.maximum(count - (STAGES - 1), 0)
    lax.fori_loop(0, steady, functools.partial(step, STAGES - 1), 0)
    lax.fori_loop(steady, count, functools.partial(step, 0), 0)

    for number, out in enumerate(outs):
        base = picks[number] * block_tiles

        def emit(tile, carry):
            out[tile] = sums[base + tile].astype(out.dtype)
            return carry

        lax.fori_loop(0, block_tiles, emit, 0, unroll=4)


def tile_products(plan, place, picks, narrow, wide, blocks, cell_tiles, row_tiles, col_bits):
    entries, group_rows, turns = plan
    parts = len(blocks)
    slots, tile_size, _ = cell_tiles.shape
    lanes = blocks[0].shape[-1]
    blocks = [block.reshape(-1, tile_size, lanes) for block in blocks]
    block_tiles = blocks[0].shape[0]
    smem = pl.BlockSpec(memory_space=pltpu.SMEM)
    vmem = pl.BlockSpec(memory_space=pltpu.VMEM)
    hbm = pl.BlockSpec(memory_space=pltpu.HBM)
    shape = (block_tiles, tile_size, lanes)
    outs = pl.pallas_call(
        functools.partial(tile_kernel, parts=parts, col_bits=col_bits, narrow=narrow, wide=wide),
        out_shape=[jax.ShapeDtypeStruct(shape, jnp.bfloat16)] * narrow
        + [jax.ShapeDtypeStruct(shape, jnp.float32)] * wide,
        in_specs=[smem] * 5 + [vmem] * parts + [hbm],
        out_specs=[vmem] * (narrow + wide),
        scratch_shapes=[
            pltpu.VMEM((row_tiles, tile_size, lanes), jnp.float32),
            pltpu.VMEM((parts * block_tiles, tile_size, lanes), jnp.bfloat16),
            pltpu.VMEM((STAGES * BATCH + 1, tile_size, tile_size), jnp.bfloat16),
            pltpu.SemaphoreType.DMA((STAGES,)),
        ],
        cost_estimate=pl.CostEstimate(
            flops=slots * tile_size * tile_size * lanes,
            bytes_accessed=slots * tile_size * tile_size + row_tiles * tile_size * lanes,
            transcendentals=0,
        ),
        name="tile_products",
    )(entries, group_rows, turns, place, picks, *blocks, cell_tiles)
    return [out.reshape(block_tiles * tile_size, lanes) for out in outs]


def swap(value, bits):
    size = lax.axis_size("row")
    return lax.ppermute(value, "row", [(i, i ^ bits) for i in range(size)])


def gather_far(piece):
    size = lax.axis_size("row")
    if size & (size - 1):
        far = {0: piece}
        for k in range(1, size):
            far[k] = lax.ppermute(piece, "row", [(i, (i - k) % size) for i in range(size)])
        return far
    return {bits: swap(piece, bits) if bits else piece for bits in range(0, size, 2)}


def gather_near(far):
    size = lax.axis_size("row")
    pieces = dict(far)
    if size > 1 and size & (size - 1) == 0:
        for bits, value in far.items():
            pieces[bits | 1] = swap(value, 1)
    return [pieces[k] for k in range(size)]


def gather_order():
    size = lax.axis_size("row")
    own = lax.axis_index("row")
    offsets = lax.broadcasted_iota(jnp.int32, (size,), 0)
    return lax.rem(own + offsets, size) if size & (size - 1) else own ^ offsets


def disjoint(pairs):
    return len({s for s, _ in pairs}) == len(pairs) and len({t for _, t in pairs}) == len(pairs)


def both_ways(ahead, up_pairs):
    size = lax.axis_size("col")
    own = lax.axis_index("col")
    down_pairs = [(size - 1 - s, size - 1 - t) for s, t in up_pairs]
    if disjoint(up_pairs + down_pairs):
        going_up = functools.reduce(jnp.logical_or, [own == s for s, _ in up_pairs])
        return [(jnp.where(going_up, own + ahead, own - ahead), up_pairs + down_pairs)]
    return [(own + ahead, up_pairs), (own - ahead, down_pairs)]


def line_messages():
    size = lax.axis_size("col")
    inner = size - 2
    hops = [both_ways(inner + 1 - turn, [(i, i + 1) for i in range(turn + 1)]) for turn in range(inner - 1)]
    near = []
    if size > 1:
        own = lax.axis_index("col")
        near = [(own + 1, [(i, i + 1) for i in range(size - 1)]), (own - 1, [(i + 1, i) for i in range(size - 1)])]
    far = both_ways(2, [(i, i + 2) for i in range(size - 2)]) if size > 2 else []
    return hops, near, far


def line_picks():
    hops, near, far = line_messages()
    first = hops[0] if hops else far
    later = [message for turn in hops[1:] for message in turn] + (far if hops else [])
    narrow = [index for index, _ in first + near]
    wide = [index for index, _ in later] + [lax.axis_index("col")]
    last = lax.axis_size("col") - 1
    numbers = lax.broadcasted_iota(jnp.int32, (len(narrow + wide),), 0)
    picks = jnp.zeros_like(numbers)
    for number, index in enumerate(narrow + wide):
        picks = jnp.where(numbers == number, jnp.clip(index, 0, last), picks)
    return picks, len(narrow), len(wide)


def reduce_line(picked):
    hops, near, far = line_messages()
    first = len(hops[0] if hops else far)
    sent = picked[:first]
    near_sent = picked[first : first + len(near)]
    later = list(picked[first + len(near) :])

    def move(values, messages):
        return [lax.ppermute(value, "col", pairs) for value, (_, pairs) in zip(values, messages)]

    def added(messages, carried):
        values = [later.pop(0) for _ in messages]
        carried = carried * (len(values) if len(carried) < len(values) else 1)
        if len(values) < len(carried):
            carried = carried[:1]
        return [(v + c.astype(jnp.float32)).astype(jnp.bfloat16) for v, c in zip(values, carried)]

    carried = None
    for turn in hops:
        values = sent if carried is None else added(turn, carried)
        carried = move(values, turn)
    parts = move(near_sent, near)
    if far:
        values = sent if carried is None else added(far, carried)
        parts = parts + move(values, far)
    return later[0], parts


def add_parts(own, parts):
    for part in parts:
        own = own + part.astype(jnp.float32)
    return own.astype(jnp.bfloat16)


def on_device(features, tiles, tile_rows, tile_cols, valid, weight, bias):
    sub_rows, width = features.shape
    tile_size = tiles.shape[3]
    row_tiles = sub_rows * lax.axis_size("col") // tile_size
    col_tiles = sub_rows * lax.axis_size("row") // tile_size
    col_bits = (col_tiles - 1).bit_length()
    chunks = channel_chunks(width)
    plan = plan_groups(tile_rows[0, 0], tile_cols[0, 0], valid[0, 0], row_tiles, col_bits)
    picks, narrow, wide = line_picks()
    place = gather_order()
    far = []
    for start, size in chunks:
        piece = features[:, start : start + size]
        if far:
            piece, far[-1] = lax.optimization_barrier((piece, far[-1]))
        far.append(gather_far(piece))
    mixed = bias[None, :]
    for index, (start, size) in enumerate(chunks):
        blocks = gather_near(far[index])
        picked = tile_products(plan, place, picks, narrow, wide, blocks, tiles[0, 0], row_tiles, col_bits)
        own, parts = reduce_line(picked)
        aggregated = add_parts(own, parts)
        mixed = mixed + jnp.dot(aggregated, weight[start : start + size], preferred_element_type=jnp.float32)
        if index < len(chunks) - 1:
            mixed = lax.optimization_barrier(mixed)
    return jnp.maximum(mixed, 0.0).astype(jnp.bfloat16)


def solution(mesh):
    def call(features, *operands):
        step = jax.shard_map(
            on_device,
            mesh=mesh,
            in_specs=(
                P(("row", "col"), None),
                P("row", "col", None, None, None),
                P("row", "col", None),
                P("row", "col", None),
                P("row", "col", None),
                P(),
                P(),
            ),
            out_specs=P(("row", "col"), None),
            check_vma=False,
        )
        return step(features, *operands)

    return call
```

profile of v0, /device:TPU:5, one launch (start us, length us, event | category | flops | bytes accessed | tf_op | source)
XLA Modules:
  0.0 164.7 jit_solution(15258978258389234358)
XLA Ops:
  0.0 1.3 fusion.15
  1.3 1.2 collective-permute-start.2
  2.5 1.2 collective-permute-start.1
  6.8 8.3 %collective-permute-done.2 = bf16[2048,128]{1,0:T(8,128)(2,1)S(1)} collective-permute-done((bf16[2048,128]{1,0:T(8,128)(2,1)S(1)}, bf16[2048,128]{1,0:T(8,128)(2,1)S(1)}, u32[]{:S(2)}, u32[]{:S(2)}) %collective-permute-start.2) | collective-permute-done | bytes 524320 | tf_op jit(solution)/shard_map/ppermute | solution.py:148
  15.1 12.2 %collective-permute-done.1 = bf16[2048,128]{1,0:T(8,128)(2,1)S(1)} collective-permute-done((bf16[2048,128]{1,0:T(8,128)(2,1)S(1)}, bf16[2048,128]{1,0:T(8,128)(2,1)S(1)}, u32[]{:S(2)}, u32[]{:S(2)}) %collective-permute-start.1) | collective-permute-done | bytes 524320 | tf_op jit(solution)/shard_map/ppermute | solution.py:148
  30.4 1.2 collective-permute-start.16
  32.1 1.1 collective-permute-start.12
  33.1 1.3 collective-permute-start.5
  36.6 7.9 %collective-permute-done.16 = bf16[2048,128]{1,0:T(8,128)(2,1)} collective-permute-done((bf16[2048,128]{1,0:T(8,128)(2,1)S(1)}, bf16[2048,128]{1,0:T(8,128)(2,1)}, u32[]{:S(2)}, u32[]{:S(2)}) %collective-permute-start.16) | collective-permute-done | bytes 524320 | tf_op jit(solution)/shard_map/ppermute | solution.py:148
  44.6 2.2 %collective-permute-start.17 = (bf16[2048,128]{1,0:T(8,128)(2,1)}, bf16[2048,128]{1,0:T(8,128)(2,1)}, u32[]{:S(2)}, u32[]{:S(2)}) collective-permute-start(bf16[2048,128]{1,0:T(8,128)(2,1)} %collective-permute-done.16), channel_id=1, source_target_pairs={{0,4},{4,0},{8,12},{12,8},{16,20},{20,16},{24,28},{28,24},{1,5},{5... | collective-permute-start | bytes 1572872 | tf_op jit(solution)/shard_map/ppermute | solution.py:148
  46.8 9.8 %collective-permute-done.14 = bf16[2048,128]{1,0:T(8,128)(2,1)} collective-permute-done((bf16[2048,128]{1,0:T(8,128)(2,1)S(1)}, bf16[2048,128]{1,0:T(8,128)(2,1)}, u32[]{:S(2)}, u32[]{:S(2)}) %collective-permute-start.14) | collective-permute-done | bytes 524320 | tf_op jit(solution)/shard_map/ppermute | solution.py:148
  57.2 10.3 %tile_products.2 = (bf16[16,128,128]{2,1,0:T(8,128)(2,1)}, bf16[16,128,128]{2,1,0:T(8,128)(2,1)}, bf16[16,128,128]{2,1,0:T(8,128)(2,1)}, f32[16,128,128]{2,1,0:T(8,128)}, f32[16,128,128]{2,1,0:T(8,128)}) custom-call(s32[832]{0:T(1024)} %broadcast_add_fusion.entries, s32[416]{0:T(512)} %broadcast_minimum_fusion.group_rows, s32[1]{0:T(128)} %bitcast.turns, ...), custom_call_target="tpu_custom_call" | custom-call | flops 1610612736 | bytes 13631488 | tf_op jit(solution)/shard_map/tile_products/pallas_call | solution.py:124
  67.5 1.3 collective-permute-start.9
  68.9 10.4 %tile_products.3 = (bf16[16,128,128]{2,1,0:T(8,128)(2,1)}, bf16[16,128,128]{2,1,0:T(8,128)(2,1)}, bf16[16,128,128]{2,1,0:T(8,128)(2,1)}, f32[16,128,128]{2,1,0:T(8,128)}, f32[16,128,128]{2,1,0:T(8,128)}) custom-call(s32[832]{0:T(1024)} %broadcast_add_fusion.entries, s32[416]{0:T(512)} %broadcast_minimum_fusion.group_rows, s32[1]{0:T(128)} %bitcast.turns, ...), custom_call_target="tpu_custom_call" | custom-call | flops 1610612736 | bytes 13631488 | tf_op jit(solution)/shard_map/tile_products/pallas_call | solution.py:124
  79.4 1.5 collective-permute-start.20
  80.8 1.3 collective-permute-start.7
  82.2 1.3 collective-permute-start.8
  83.6 11.0 %collective-permute-start.10 = (bf16[2048,128]{1,0:T(8,128)(2,1)S(1)}, bf16[2048,128]{1,0:T(8,128)(2,1)S(1)}, u32[]{:S(2)}, u32[]{:S(2)}) collective-permute-start(bf16[2048,128]{1,0:T(8,128)(2,1)S(1)} %fusion.7), channel_id=1, source_target_pairs={{0,2},{1,3},{3,1},{2,0},{4,6},{5,7},{7,5},{6,4},{8,10},{9,11},{11,... | collective-permute-start | bytes 1572872 | tf_op jit(solution)/shard_map/ppermute | solution.py:225
  94.6 3.4 %collective-permute-start.18 = (bf16[2048,128]{1,0:T(8,128)(2,1)}, bf16[2048,128]{1,0:T(8,128)(2,1)S(1)}, u32[]{:S(2)}, u32[]{:S(2)}) collective-permute-start(bf16[2048,128]{1,0:T(8,128)(2,1)} %bitcast.62), channel_id=1, source_target_pairs={{0,1},{1,2},{2,3},{4,5},{5,6},{6,7},{8,9},{9,10},{10,11},{12,13},{... | collective-permute-start | bytes 1572872 | tf_op jit(solution)/shard_map/ppermute | solution.py:225
  98.0 1.3 collective-permute-start.19
  99.5 10.2 %collective-permute-start.21 = (bf16[2048,128]{1,0:T(8,128)(2,1)S(1)}, bf16[2048,128]{1,0:T(8,128)(2,1)S(1)}, u32[]{:S(2)}, u32[]{:S(2)}) collective-permute-start(bf16[2048,128]{1,0:T(8,128)(2,1)S(1)} %fusion.3), channel_id=1, source_target_pairs={{0,2},{1,3},{3,1},{2,0},{4,6},{5,7},{7,5},{6,4},{8,10},{9,11},{11,... | collective-permute-start | bytes 1572872 | tf_op jit(solution)/shard_map/ppermute | solution.py:225
  109.7 19.6 %collective-permute-done.10 = bf16[2048,128]{1,0:T(8,128)(2,1)S(1)} collective-permute-done((bf16[2048,128]{1,0:T(8,128)(2,1)S(1)}, bf16[2048,128]{1,0:T(8,128)(2,1)S(1)}, u32[]{:S(2)}, u32[]{:S(2)}) %collective-permute-start.10) | collective-permute-done | bytes 524320 | tf_op jit(solution)/shard_map/ppermute | solution.py:225
  130.1 33.0 %collective-permute-done.21 = bf16[2048,128]{1,0:T(8,128)(2,1)S(1)} collective-permute-done((bf16[2048,128]{1,0:T(8,128)(2,1)S(1)}, bf16[2048,128]{1,0:T(8,128)(2,1)S(1)}, u32[]{:S(2)}, u32[]{:S(2)}) %collective-permute-start.21) | collective-permute-done | bytes 524320 | tf_op jit(solution)/shard_map/ppermute | solution.py:225
  163.3 1.4 fusion.1
  (74 shorter events, 9.9 us)
Async XLA Ops:
  1.3 55.9 %copy-start.1 = (bf16[2048,128]{1,0:T(8,128)(2,1)}, bf16[2048,128]{1,0:T(8,128)(2,1)S(1)}, u32[]{:S(2)}) copy-start(bf16[2048,128]{1,0:T(8,128)(2,1)S(1)} %get-tuple-element.20) | copy-start | bytes 1572868
  1.3 66.2 %copy-start = (bf16[2048,128]{1,0:T(8,128)(2,1)}, bf16[2048,128]{1,0:T(8,128)(2,1)S(1)}, u32[]{:S(2)}) copy-start(bf16[2048,128]{1,0:T(8,128)(2,1)S(1)} %get-tuple-element.29) | copy-start | bytes 1572868
  1.3 13.8 %collective-permute-start.2 = (bf16[2048,128]{1,0:T(8,128)(2,1)S(1)}, bf16[2048,128]{1,0:T(8,128)(2,1)S(1)}, u32[]{:S(2)}, u32[]{:S(2)}) collective-permute-start(bf16[2048,128]{1,0:T(8,128)(2,1)S(1)} %get-tuple-element.20), channel_id=1, source_target_pairs={{0,24},{4,28},{8,16},{12,20},{16,8},{20,12},{24,0},{28,4},{1,25},{... | collective-permute-start | bytes 1572872 | tf_op jit(solution)/shard_map/ppermute | solution.py:148
  2.5 24.8 %collective-permute-start.1 = (bf16[2048,128]{1,0:T(8,128)(2,1)S(1)}, bf16[2048,128]{1,0:T(8,128)(2,1)S(1)}, u32[]{:S(2)}, u32[]{:S(2)}) collective-permute-start(bf16[2048,128]{1,0:T(8,128)(2,1)S(1)} %get-tuple-element.20), channel_id=1, source_target_pairs={{0,16},{4,20},{8,24},{12,28},{16,0},{20,4},{24,8},{28,12},{1,17},{... | collective-permute-start | bytes 1572872 | tf_op jit(solution)/shard_map/ppermute | solution.py:148
  3.8 23.6 %collective-permute-start = (bf16[2048,128]{1,0:T(8,128)(2,1)S(1)}, bf16[2048,128]{1,0:T(8,128)(2,1)S(1)}, u32[]{:S(2)}, u32[]{:S(2)}) collective-permute-start(bf16[2048,128]{1,0:T(8,128)(2,1)S(1)} %get-tuple-element.20), channel_id=1, source_target_pairs={{0,8},{4,12},{8,0},{12,4},{16,24},{20,28},{24,16},{28,20},{1,9},{5... | collective-permute-start | bytes 1572872 | tf_op jit(solution)/shard_map/ppermute | solution.py:148
  27.3 5.8 %collective-permute-start.3 = (bf16[2048,128]{1,0:T(8,128)(2,1)S(1)}, bf16[2048,128]{1,0:T(8,128)(2,1)S(1)}, u32[]{:S(2)}, u32[]{:S(2)}) collective-permute-start(bf16[2048,128]{1,0:T(8,128)(2,1)S(1)} %get-tuple-element.20), channel_id=1, source_target_pairs={{0,4},{4,0},{8,12},{12,8},{16,20},{20,16},{24,28},{28,24},{1,5},{5... | collective-permute-start | bytes 1572872 | tf_op jit(solution)/shard_map/ppermute | solution.py:148
  27.9 6.5 %collective-permute-start.4 = (bf16[2048,128]{1,0:T(8,128)(2,1)S(1)}, bf16[2048,128]{1,0:T(8,128)(2,1)}, u32[]{:S(2)}, u32[]{:S(2)}) collective-permute-start(bf16[2048,128]{1,0:T(8,128)(2,1)S(1)} %collective-permute-done), channel_id=1, source_target_pairs={{0,4},{4,0},{8,12},{12,8},{16,20},{20,16},{24,28},{28,24},{1,5},{5... | collective-permute-start | bytes 1572872 | tf_op jit(solution)/shard_map/ppermute | solution.py:148
  30.4 14.2 %collective-permute-start.16 = (bf16[2048,128]{1,0:T(8,128)(2,1)S(1)}, bf16[2048,128]{1,0:T(8,128)(2,1)}, u32[]{:S(2)}, u32[]{:S(2)}) collective-permute-start(bf16[2048,128]{1,0:T(8,128)(2,1)S(1)} %get-tuple-element.29), channel_id=1, source_target_pairs={{0,24},{4,28},{8,16},{12,20},{16,8},{20,12},{24,0},{28,4},{1,25},{... | collective-permute-start | bytes 1572872 | tf_op jit(solution)/shard_map/ppermute | solution.py:148
  31.6 24.9 %collective-permute-start.14 = (bf16[2048,128]{1,0:T(8,128)(2,1)S(1)}, bf16[2048,128]{1,0:T(8,128)(2,1)}, u32[]{:S(2)}, u32[]{:S(2)}) collective-permute-start(bf16[2048,128]{1,0:T(8,128)(2,1)S(1)} %get-tuple-element.29), channel_id=1, source_target_pairs={{0,16},{4,20},{8,24},{12,28},{16,0},{20,4},{24,8},{28,12},{1,17},{... | collective-permute-start | bytes 1572872 | tf_op jit(solution)/shard_map/ppermute | solution.py:148
  32.1 25.0 %collective-permute-start.12 = (bf16[2048,128]{1,0:T(8,128)(2,1)S(1)}, bf16[2048,128]{1,0:T(8,128)(2,1)}, u32[]{:S(2)}, u32[]{:S(2)}) collective-permute-start(bf16[2048,128]{1,0:T(8,128)(2,1)S(1)} %get-tuple-element.29), channel_id=1, source_target_pairs={{0,8},{4,12},{8,0},{12,4},{16,24},{20,28},{24,16},{28,20},{1,9},{5... | collective-permute-start | bytes 1572872 | tf_op jit(solution)/shard_map/ppermute | solution.py:148
  33.1 3.1 %collective-permute-start.5 = (bf16[2048,128]{1,0:T(8,128)(2,1)S(1)}, bf16[2048,128]{1,0:T(8,128)(2,1)S(1)}, u32[]{:S(2)}, u32[]{:S(2)}) collective-permute-start(bf16[2048,128]{1,0:T(8,128)(2,1)S(1)} %collective-permute-done.1), channel_id=1, source_target_pairs={{0,4},{4,0},{8,12},{12,8},{16,20},{20,16},{24,28},{28,24},{1,5},{5... | collective-permute-start | bytes 1572872 | tf_op jit(solution)/shard_map/ppermute | solution.py:148
  34.4 22.7 %collective-permute-start.6 = (bf16[2048,128]{1,0:T(8,128)(2,1)S(1)}, bf16[2048,128]{1,0:T(8,128)(2,1)}, u32[]{:S(2)}, u32[]{:S(2)}) collective-permute-start(bf16[2048,128]{1,0:T(8,128)(2,1)S(1)} %collective-permute-done.2), channel_id=1, source_target_pairs={{0,4},{4,0},{8,12},{12,8},{16,20},{20,16},{24,28},{28,24},{1,5},{5... | collective-permute-start | bytes 1572872 | tf_op jit(solution)/shard_map/ppermute | solution.py:148
  36.2 32.6 %collective-permute-start.11 = (bf16[2048,128]{1,0:T(8,128)(2,1)S(1)}, bf16[2048,128]{1,0:T(8,128)(2,1)}, u32[]{:S(2)}, u32[]{:S(2)}) collective-permute-start(bf16[2048,128]{1,0:T(8,128)(2,1)S(1)} %get-tuple-element.29), channel_id=1, source_target_pairs={{0,4},{4,0},{8,12},{12,8},{16,20},{20,16},{24,28},{28,24},{1,5},{5... | collective-permute-start | bytes 1572872 | tf_op jit(solution)/shard_map/ppermute | solution.py:148
  44.6 24.3 %collective-permute-start.17 = (bf16[2048,128]{1,0:T(8,128)(2,1)}, bf16[2048,128]{1,0:T(8,128)(2,1)}, u32[]{:S(2)}, u32[]{:S(2)}) collective-permute-start(bf16[2048,128]{1,0:T(8,128)(2,1)} %collective-permute-done.16), channel_id=1, source_target_pairs={{0,4},{4,0},{8,12},{12,8},{16,20},{20,16},{24,28},{28,24},{1,5},{5... | collective-permute-start | bytes 1572872 | tf_op jit(solution)/shard_map/ppermute | solution.py:148
  56.6 12.3 %collective-permute-start.15 = (bf16[2048,128]{1,0:T(8,128)(2,1)}, bf16[2048,128]{1,0:T(8,128)(2,1)}, u32[]{:S(2)}, u32[]{:S(2)}) collective-permute-start(bf16[2048,128]{1,0:T(8,128)(2,1)} %collective-permute-done.14), channel_id=1, source_target_pairs={{0,4},{4,0},{8,12},{12,8},{16,20},{20,16},{24,28},{28,24},{1,5},{5... | collective-permute-start | bytes 1572872 | tf_op jit(solution)/shard_map/ppermute | solution.py:148
  57.1 11.8 %collective-permute-start.13 = (bf16[2048,128]{1,0:T(8,128)(2,1)}, bf16[2048,128]{1,0:T(8,128)(2,1)}, u32[]{:S(2)}, u32[]{:S(2)}) collective-permute-start(bf16[2048,128]{1,0:T(8,128)(2,1)} %collective-permute-done.12), channel_id=1, source_target_pairs={{0,4},{4,0},{8,12},{12,8},{16,20},{20,16},{24,28},{28,24},{1,5},{5... | collective-permute-start | bytes 1572872 | tf_op jit(solution)/shard_map/ppermute | solution.py:148
  67.5 16.0 %collective-permute-start.9 = (bf16[2048,128]{1,0:T(8,128)(2,1)}, bf16[2048,128]{1,0:T(8,128)(2,1)S(1)}, u32[]{:S(2)}, u32[]{:S(2)}) collective-permute-start(bf16[2048,128]{1,0:T(8,128)(2,1)} %bitcast.63), channel_id=1, source_target_pairs={{0,1},{3,2},{4,5},{7,6},{8,9},{11,10},{12,13},{15,14},{16,17},{19,... | collective-permute-start | bytes 1572872 | tf_op jit(solution)/shard_map/ppermute | solution.py:225
  79.4 18.6 %collective-permute-start.20 = (bf16[2048,128]{1,0:T(8,128)(2,1)}, bf16[2048,128]{1,0:T(8,128)(2,1)S(1)}, u32[]{:S(2)}, u32[]{:S(2)}) collective-permute-start(bf16[2048,128]{1,0:T(8,128)(2,1)} %bitcast.64), channel_id=1, source_target_pairs={{0,1},{3,2},{4,5},{7,6},{8,9},{11,10},{12,13},{15,14},{16,17},{19,... | collective-permute-start | bytes 1572872 | tf_op jit(solution)/shard_map/ppermute | solution.py:225
  80.8 18.6 %collective-permute-start.7 = (bf16[2048,128]{1,0:T(8,128)(2,1)S(1)}, bf16[2048,128]{1,0:T(8,128)(2,1)S(1)}, u32[]{:S(2)}, u32[]{:S(2)}) collective-permute-start(bf16[2048,128]{1,0:T(8,128)(2,1)S(1)} %bitcast.60), channel_id=1, source_target_pairs={{0,1},{1,2},{2,3},{4,5},{5,6},{6,7},{8,9},{9,10},{10,11},{12,13},{... | collective-permute-start | bytes 1572872 | tf_op jit(solution)/shard_map/ppermute | solution.py:225
  82.2 27.5 %collective-permute-start.8 = (bf16[2048,128]{1,0:T(8,128)(2,1)S(1)}, bf16[2048,128]{1,0:T(8,128)(2,1)S(1)}, u32[]{:S(2)}, u32[]{:S(2)}) collective-permute-start(bf16[2048,128]{1,0:T(8,128)(2,1)S(1)} %bitcast.59), channel_id=1, source_target_pairs={{1,0},{2,1},{3,2},{5,4},{6,5},{7,6},{9,8},{10,9},{11,10},{13,12},{... | collective-permute-start | bytes 1572872 | tf_op jit(solution)/shard_map/ppermute | solution.py:225
  83.6 45.7 %collective-permute-start.10 = (bf16[2048,128]{1,0:T(8,128)(2,1)S(1)}, bf16[2048,128]{1,0:T(8,128)(2,1)S(1)}, u32[]{:S(2)}, u32[]{:S(2)}) collective-permute-start(bf16[2048,128]{1,0:T(8,128)(2,1)S(1)} %fusion.7), channel_id=1, source_target_pairs={{0,2},{1,3},{3,1},{2,0},{4,6},{5,7},{7,5},{6,4},{8,10},{9,11},{11,... | collective-permute-start | bytes 1572872 | tf_op jit(solution)/shard_map/ppermute | solution.py:225
  94.6 35.5 %collective-permute-start.18 = (bf16[2048,128]{1,0:T(8,128)(2,1)}, bf16[2048,128]{1,0:T(8,128)(2,1)S(1)}, u32[]{:S(2)}, u32[]{:S(2)}) collective-permute-start(bf16[2048,128]{1,0:T(8,128)(2,1)} %bitcast.62), channel_id=1, source_target_pairs={{0,1},{1,2},{2,3},{4,5},{5,6},{6,7},{8,9},{9,10},{10,11},{12,13},{... | collective-permute-start | bytes 1572872 | tf_op jit(solution)/shard_map/ppermute | solution.py:225
  98.0 32.0 %collective-permute-start.19 = (bf16[2048,128]{1,0:T(8,128)(2,1)}, bf16[2048,128]{1,0:T(8,128)(2,1)S(1)}, u32[]{:S(2)}, u32[]{:S(2)}) collective-permute-start(bf16[2048,128]{1,0:T(8,128)(2,1)} %bitcast.61), channel_id=1, source_target_pairs={{1,0},{2,1},{3,2},{5,4},{6,5},{7,6},{9,8},{10,9},{11,10},{13,12},{... | collective-permute-start | bytes 1572872 | tf_op jit(solution)/shard_map/ppermute | solution.py:225
  99.5 63.6 %collective-permute-start.21 = (bf16[2048,128]{1,0:T(8,128)(2,1)S(1)}, bf16[2048,128]{1,0:T(8,128)(2,1)S(1)}, u32[]{:S(2)}, u32[]{:S(2)}) collective-permute-start(bf16[2048,128]{1,0:T(8,128)(2,1)S(1)} %fusion.3), channel_id=1, source_target_pairs={{0,2},{1,3},{3,1},{2,0},{4,6},{5,7},{7,5},{6,4},{8,10},{9,11},{11,... | collective-permute-start | bytes 1572872 | tf_op jit(solution)/shard_map/ppermute | solution.py:225
  (13 other events, 350.6 us)
where the time goes:
time: 166 us; the launch traced here: 165 us
  waiting for transfers between devices  90.9 us (55%)
  starting transfers between devices  41.9 us (25%)
  Pallas kernels  20.7 us (12%)
  other arithmetic  6.96 us (4%)
  matrix products  1.79 us (1%)
    ppermute x8, waiting for transfers between devices, move(): lax.ppermute(value, 'col', pairs)  52.7 us
    ppermute x14, waiting for transfers between devices, swap(): return lax.ppermute(value, 'row', [(i, i ^ bits) for i in range(size)])  38.3 us
    ppermute x8, starting transfers between devices, move(): lax.ppermute(value, 'col', pairs)  31.3 us
    pallas_call x2, Pallas kernels, tile_products(): pl.pallas_call(functools.partial(tile_kernel, parts=parts, col_bits=col_b...  20.7 us
    ppermute x14, starting transfers between devices, swap(): return lax.ppermute(value, 'row', [(i, i ^ bits) for i in range(size)])  10.6 us
  transfers between devices with their start and end apart: 22, of which 6 were waited for; matrix products, arithmetic and copies ran while one was open for 4% of the time, Pallas kernels for 13%

commit v1 on v0

--- a/solution.py
+++ b/solution.py
@@ -12,6 +12,8 @@
 GROUP = 2
 UNROLL = 16
 STAGES = 4
+VMEM_LIMIT = 44 * 1024 * 1024
+KEPT_ROOM = 6
 BATCH = GROUP * UNROLL
 
 
@@ -20,9 +22,8 @@
     return [(start, lanes) for start in range(0, width, lanes)]
 
 
-def plan_groups(cell_rows, cell_cols, cell_valid, row_tiles, col_bits):
+def plan_groups(cell_rows, cell_cols, live, row_tiles, col_bits):
     slots = cell_rows.shape[0]
-    live = cell_valid > 0
     row_ids = jnp.arange(row_tiles, dtype=jnp.int32)
     slot_ids = jnp.arange(slots, dtype=jnp.int32)
     hits = (cell_rows[:, None] == row_ids[None, :]) & live[:, None]
@@ -45,46 +46,44 @@
     return entries, group_rows, turns.reshape(1)
 
 
-def tile_kernel(entries, group_rows, turns, place, picks, *refs, parts, col_bits, narrow, wide):
-    blocks = refs[:parts]
-    tiles = refs[parts]
-    outs = refs[parts + 1 : parts + 1 + narrow + wide]
-    sums, panel, ring, tile_sems = refs[parts + 1 + narrow + wide :]
-    block_tiles = panel.shape[0] // parts
-    count = turns[0]
+def tile_kernel(*refs, lists, parts, begun, keep, col_bits, narrow, wide):
+    plans = [refs[3 * k : 3 * k + 3] for k in range(lists)]
+    place, picks = refs[3 * lists : 3 * lists + 2]
+    refs = refs[3 * lists + 2 :]
+    blocks = refs[: len(parts)]
+    tiles = refs[len(parts)]
+    started = refs[len(parts) + 1] if begun else None
+    outs = refs[len(parts) + 1 + begun :][: narrow + wide + keep]
+    sums, panel, ring, tile_sems, whole_sem, *earlier = refs[len(parts) + 1 + begun + narrow + wide + keep :]
+    block_tiles = blocks[0].shape[0]
     zero_seat = STAGES * BATCH
-
-    def fetch(turn, seats=range(BATCH)):
+    spare = place[parts[0]] * block_tiles
+
+    def fetch(entries, turn, seats=range(BATCH)):
         stage = lax.rem(turn, STAGES)
         for seat in seats:
             slot = lax.shift_right_logical(jnp.maximum(entries[turn * BATCH + seat], 0), col_bits)
             pltpu.make_async_copy(tiles.at[slot], ring.at[stage * BATCH + seat], tile_sems.at[stage]).start()
 
-    def arrive(turn):
+    def first_fetches(entries, count):
+        lax.fori_loop(0, jnp.minimum(count, STAGES - 1), lambda turn, carry: fetch(entries, turn) or carry, 0)
+
+    def step(ahead, entries, group_rows, turn, carry):
         stage = lax.rem(turn, STAGES)
+        base = stage * BATCH
         pltpu.make_async_copy(
-            tiles.at[pl.ds(0, BATCH)], ring.at[pl.ds(stage * BATCH, BATCH)], tile_sems.at[stage]
+            tiles.at[pl.ds(0, BATCH)], ring.at[pl.ds(base, BATCH)], tile_sems.at[stage]
         ).wait()
-
-    lax.fori_loop(0, jnp.minimum(count, STAGES - 1), lambda turn, carry: fetch(turn) or carry, 0)
-    ring[zero_seat] = jnp.zeros(ring.shape[1:], ring.dtype)
-    sums[...] = jnp.zeros(sums.shape, sums.dtype)
-    for part in range(parts):
-        panel[pl.ds(place[part] * block_tiles, block_tiles)] = blocks[part][...]
-
-    def step(ahead, turn, carry):
-        base = lax.rem(turn, STAGES) * BATCH
-        arrive(turn)
         products = []
         for group in range(UNROLL):
             if ahead:
-                fetch(turn + ahead, range(group * GROUP, (group + 1) * GROUP))
+                fetch(entries, turn + ahead, range(group * GROUP, (group + 1) * GROUP))
             left, right = [], []
             for member in range(GROUP):
                 seat = group * GROUP + member
                 entry = entries[turn * BATCH + seat]
                 left.append(ring[jnp.where(entry < 0, zero_seat, base + seat)])
-                right.append(panel[jnp.maximum(entry, 0) & ((1 << col_bits) - 1)])
+                right.append(panel[jnp.where(entry < 0, spare, entry & ((1 << col_bits) - 1))])
             products.append(
                 jnp.dot(
                     jnp.concatenate(left, axis=1),
@@ -96,51 +95,96 @@
             sums[group_rows[turn * UNROLL + group]] += products[group]
         return carry
 
-    steady = jnp.maximum(count - (STAGES - 1), 0)
-    lax.fori_loop(0, steady, functools.partial(step, STAGES - 1), 0)
-    lax.fori_loop(steady, count, functools.partial(step, 0), 0)
-
+    first_fetches(plans[0][0], plans[0][2][0])
+    ring[zero_seat] = jnp.zeros(ring.shape[1:], ring.dtype)
+    if begun:
+        restore = pltpu.make_async_copy(started.at[pl.ds(0, sums.shape[0])], earlier[0], whole_sem)
+        restore.start()
+    sums[...] = jnp.zeros(sums.shape, sums.dtype)
+    for number, part in enumerate(parts):
+        panel[pl.ds(place[part] * block_tiles, block_tiles)] = blocks[number][...]
+    for number, (entries, group_rows, turns) in enumerate(plans):
+        count = turns[0]
+        if number:
+            first_fetches(entries, count)
+        steady = jnp.maximum(count - (STAGES - 1), 0)
+        lax.fori_loop(0, steady, functools.partial(step, STAGES - 1, entries, group_rows), 0)
+        lax.fori_loop(steady, count, functools.partial(step, 0, entries, group_rows), 0)
+
+    if keep:
+        save = pltpu.make_async_copy(sums, outs[0].at[pl.ds(0, sums.shape[0])], whole_sem)
+        save.start()
+        save.wait()
+        return
+    if begun:
+        restore.wait()
     for number, out in enumerate(outs):
         base = picks[number] * block_tiles
 
         def emit(tile, carry):
-            out[tile] = sums[base + tile].astype(out.dtype)
+            value = sums[base + tile]
+            if begun:
+                value = value + earlier[0][base + tile]
+            out[tile] = value.astype(out.dtype)
             return carry
 
         lax.fori_loop(0, block_tiles, emit, 0, unroll=4)
 
 
-def tile_products(plan, place, picks, narrow, wide, blocks, cell_tiles, row_tiles, col_bits):
-    entries, group_rows, turns = plan
-    parts = len(blocks)
+def tile_products(plans, place, picks, narrow, wide, blocks, cell_tiles, row_tiles, col_bits, begun=None, keep=False):
+    parts = sorted(blocks)
     slots, tile_size, _ = cell_tiles.shape
-    lanes = blocks[0].shape[-1]
-    blocks = [block.reshape(-1, tile_size, lanes) for block in blocks]
-    block_tiles = blocks[0].shape[0]
+    lanes = blocks[parts[0]].shape[-1]
+    values = [blocks[part].reshape(-1, tile_size, lanes) for part in parts]
+    block_tiles = values[0].shape[0]
+    if keep:
+        narrow = wide = 0
     smem = pl.BlockSpec(memory_space=pltpu.SMEM)
     vmem = pl.BlockSpec(memory_space=pltpu.VMEM)
     hbm = pl.BlockSpec(memory_space=pltpu.HBM)
     shape = (block_tiles, tile_size, lanes)
+    total = jax.ShapeDtypeStruct((row_tiles, tile_size, lanes), jnp.float32)
+    operands = [array for plan in plans for array in plan] + [place, picks] + values + [cell_tiles]
+    in_specs = [smem] * (3 * len(plans) + 2) + [vmem] * len(values) + [hbm]
+    if begun is not None:
+        operands.append(begun)
+        in_specs.append(hbm)
+    sums = pltpu.VMEM(total.shape, total.dtype)
+    scratch = [
+        sums,
+        pltpu.VMEM((1 << col_bits, tile_size, lanes), jnp.bfloat16),
+        pltpu.VMEM((STAGES * BATCH + 1, tile_size, tile_size), jnp.bfloat16),
+        pltpu.SemaphoreType.DMA((STAGES,)),
+        pltpu.SemaphoreType.DMA(()),
+    ] + [sums] * (begun is not None)
     outs = pl.pallas_call(
-        functools.partial(tile_kernel, parts=parts, col_bits=col_bits, narrow=narrow, wide=wide),
+        functools.partial(
+            tile_kernel,
+            lists=len(plans),
+            parts=parts,
+            begun=int(begun is not None),
+            keep=int(keep),
+            col_bits=col_bits,
+            narrow=narrow,
+            wide=wide,
+        ),
         out_shape=[jax.ShapeDtypeStruct(shape, jnp.bfloat16)] * narrow
-        + [jax.ShapeDtypeStruct(shape, jnp.float32)] * wide,
-        in_specs=[smem] * 5 + [vmem] * parts + [hbm],
-        out_specs=[vmem] * (narrow + wide),
-        scratch_shapes=[
-            pltpu.VMEM((row_tiles, tile_size, lanes), jnp.float32),
-            pltpu.VMEM((parts * block_tiles, tile_size, lanes), jnp.bfloat16),
-            pltpu.VMEM((STAGES * BATCH + 1, tile_size, tile_size), jnp.bfloat16),
-            pltpu.SemaphoreType.DMA((STAGES,)),
-        ],
+        + [jax.ShapeDtypeStruct(shape, jnp.float32)] * wide
+        + [jax.ShapeDtypeStruct((KEPT_ROOM * row_tiles, tile_size, lanes), jnp.float32)] * keep,
+        in_specs=in_specs,
+        out_specs=[hbm if keep else vmem] * (narrow + wide + keep),
+        scratch_shapes=scratch,
+        compiler_params=pltpu.CompilerParams(vmem_limit_bytes=VMEM_LIMIT),
         cost_estimate=pl.CostEstimate(
             flops=slots * tile_size * tile_size * lanes,
             bytes_accessed=slots * tile_size * tile_size + row_tiles * tile_size * lanes,
             transcendentals=0,
         ),
         name="tile_products",
-    )(entries, group_rows, turns, place, picks, *blocks, cell_tiles)
-    return [out.reshape(block_tiles * tile_size, lanes) for out in outs]
+    )(*operands)
+    if keep:
+        return outs[0]
+    return [out.reshape(block_tiles * tile_size, lanes) for out in outs[: narrow + wide]]
 
 
 def swap(value, bits):
@@ -148,14 +192,21 @@
     return lax.ppermute(value, "row", [(i, i ^ bits) for i in range(size)])
 
 
+def late_offset():
+    size = lax.axis_size("row")
+    return size - 2 if size > 2 and size & (size - 1) == 0 else None
+
+
 def gather_far(piece):
     size = lax.axis_size("row")
+    far = {0: piece}
     if size & (size - 1):
-        far = {0: piece}
         for k in range(1, size):
             far[k] = lax.ppermute(piece, "row", [(i, (i - k) % size) for i in range(size)])
         return far
-    return {bits: swap(piece, bits) if bits else piece for bits in range(0, size, 2)}
+    for bits in range(2, size, 2):
+        far[bits] = swap(piece, bits)
+    return far
 
 
 def gather_near(far):
@@ -164,7 +215,7 @@
     if size > 1 and size & (size - 1) == 0:
         for bits, value in far.items():
             pieces[bits | 1] = swap(value, 1)
-    return [pieces[k] for k in range(size)]
+    return pieces
 
 
 def gather_order():
@@ -255,19 +306,32 @@
     col_tiles = sub_rows * lax.axis_size("row") // tile_size
     col_bits = (col_tiles - 1).bit_length()
     chunks = channel_chunks(width)
-    plan = plan_groups(tile_rows[0, 0], tile_cols[0, 0], valid[0, 0], row_tiles, col_bits)
+    late = late_offset()
+    cell_rows, cell_cols, live = tile_rows[0, 0], tile_cols[0, 0], valid[0, 0] > 0
     picks, narrow, wide = line_picks()
     place = gather_order()
+    lives = [live]
+    if late is not None:
+        offset = (cell_cols // (sub_rows // tile_size)) ^ lax.axis_index("row")
+        after = (offset | 1) == (late | 1)
+        lives = [live & ~after, live & after]
+    plans = [plan_groups(cell_rows, cell_cols, part, row_tiles, col_bits) for part in lives]
     far = []
     for start, size in chunks:
-        piece = features[:, start : start + size]
-        if far:
-            piece, far[-1] = lax.optimization_barrier((piece, far[-1]))
-        far.append(gather_far(piece))
+        far.append(gather_far(features[:, start : start + size]))
+    products = functools.partial(
+        tile_products, cell_tiles=tiles[0, 0], row_tiles=row_tiles, col_bits=col_bits, place=place, picks=picks
+    )
     mixed = bias[None, :]
     for index, (start, size) in enumerate(chunks):
+        begun, used = None, plans
+        if index == 0 and late is not None:
+            blocks = gather_near({bits: far[0][bits] for bits in far[0] if bits != late})
+            begun = products(plans[:1], narrow=narrow, wide=wide, blocks=blocks, keep=True)
+            used = plans[1:]
+            far[0] = {late: far[0][late]}
         blocks = gather_near(far[index])
-        picked = tile_products(plan, place, picks, narrow, wide, blocks, tiles[0, 0], row_tiles, col_bits)
+        picked = products(used, narrow=narrow, wide=wide, blocks=blocks, begun=begun)
         own, parts = reduce_line(picked)
         aggregated = add_parts(own, parts)
         mixed = mixed + jnp.dot(aggregated, weight[start : start + size], preferred_element_type=jnp.float32)

time: 166 us -> 165 us (level)
  the two profiles are of different devices: /device:TPU:5 before, /device:TPU:0 now
where the time goes in v1:
time: 165 us; the launch traced here: 162 us
  waiting for transfers between devices  92.6 us (56%)
  starting transfers between devices  29.6 us (18%)
  Pallas kernels  29 us (18%)
  other arithmetic  6.36 us (4%)
  matrix products  1.81 us (1%)
  between operations  1.71 us (1%)
    ppermute x8, waiting for transfers between devices, move(): lax.ppermute(value, 'col', pairs)  58.4 us
    ppermute x14, waiting for transfers between devices, swap(): return lax.ppermute(value, 'row', [(i, i ^ bits) for i in range(size)])  34.2 us
    pallas_call x3, Pallas kernels, tile_products(): pl.pallas_call(functools.partial(tile_kernel, lists=len(plans), parts=par...  29 us
    ppermute x8, starting transfers between devices, move(): lax.ppermute(value, 'col', pairs)  18 us
    ppermute x14, starting transfers between devices, swap(): return lax.ppermute(value, 'row', [(i, i ^ bits) for i in range(size)])  11.6 us
  transfers between devices with their start and end apart: 22, of which 6 were waited for; matrix products, arithmetic and copies ran while one was open for 4% of the time, Pallas kernels for 18%

profile of v1, /device:TPU:0, one launch (start us, length us, event | category | flops | bytes accessed | tf_op | source)
XLA Modules:
  0.0 162.3 jit_solution(2502275021373874704)
XLA Ops:
  0.0 1.3 fusion.25
  1.3 4.0 %collective-permute-start.16 = (bf16[2048,128]{1,0:T(8,128)(2,1)S(1)}, bf16[2048,128]{1,0:T(8,128)(2,1)S(1)}, u32[]{:S(2)}, u32[]{:S(2)}) collective-permute-start(bf16[2048,128]{1,0:T(8,128)(2,1)S(1)} %get-tuple-element.37), channel_id=1, source_target_pairs={{0,24},{4,28},{8,16},{12,20},{16,8},{20,12},{24,0},{28,4},{1,25},{... | collective-permute-start | bytes 1572872 | tf_op jit(solution)/shard_map/ppermute | solution.py:192
  5.8 1.5 collective-permute-start.5
  7.8 1.4 collective-permute-start
  13.2 0.7 fusion.22
  14.9 3.2 %collective-permute-done.16 = bf16[2048,128]{1,0:T(8,128)(2,1)S(1)} collective-permute-done((bf16[2048,128]{1,0:T(8,128)(2,1)S(1)}, bf16[2048,128]{1,0:T(8,128)(2,1)S(1)}, u32[]{:S(2)}, u32[]{:S(2)}) %collective-permute-start.16) | collective-permute-done | bytes 524320 | tf_op jit(solution)/shard_map/ppermute | solution.py:192
  18.1 2.0 %collective-permute-start.12 = (bf16[2048,128]{1,0:T(8,128)(2,1)S(1)}, bf16[2048,128]{1,0:T(8,128)(2,1)S(1)}, u32[]{:S(2)}, u32[]{:S(2)}) collective-permute-start(bf16[2048,128]{1,0:T(8,128)(2,1)S(1)} %get-tuple-element.37), channel_id=1, source_target_pairs={{0,8},{4,12},{8,0},{12,4},{16,24},{20,28},{24,16},{28,20},{1,9},{5... | collective-permute-start | bytes 1572872 | tf_op jit(solution)/shard_map/ppermute | solution.py:192
  20.0 9.3 %collective-permute-done.14 = bf16[2048,128]{1,0:T(8,128)(2,1)S(1)} collective-permute-done((bf16[2048,128]{1,0:T(8,128)(2,1)S(1)}, bf16[2048,128]{1,0:T(8,128)(2,1)S(1)}, u32[]{:S(2)}, u32[]{:S(2)}) %collective-permute-start.14) | collective-permute-done | bytes 524320 | tf_op jit(solution)/shard_map/ppermute | solution.py:192
  29.4 21.6 %collective-permute-done.5 = bf16[2048,128]{1,0:T(8,128)(2,1)} collective-permute-done((bf16[2048,128]{1,0:T(8,128)(2,1)S(1)}, bf16[2048,128]{1,0:T(8,128)(2,1)}, u32[]{:S(2)}, u32[]{:S(2)}) %collective-permute-start.5) | collective-permute-done | bytes 524320 | tf_op jit(solution)/shard_map/ppermute | solution.py:192
  54.2 11.1 %tile_products.3.refs_8_ = f32[384,128,128]{2,1,0:T(8,128)} custom-call(s32[832]{0:T(1024)S(1)} %broadcast_add_fusion.refs_0_, s32[416]{0:T(512)S(1)} %get-tuple-element.41.refs_1_, s32[1]{0:T(128)} %bitcast.4.refs_2_, s32[8]{0:T(128)S(1)} %iota_xor_fusion.refs_3_.refs_6_, s32[5]{0:T(128)S(1)} %compare_select_fusion.4.refs_4_.refs_7_, ...), custom_call_target="tpu_custom_call" | custom-call | flops 1610612736 | bytes 13631488 | tf_op jit(solution)/shard_map/tile_products/pallas_call | solution.py:160
  65.3 5.9 %tile_products.4 = (bf16[16,128,128]{2,1,0:T(8,128)(2,1)S(1)}, bf16[16,128,128]{2,1,0:T(8,128)(2,1)S(1)}, bf16[16,128,128]{2,1,0:T(8,128)(2,1)S(1)}, f32[16,128,128]{2,1,0:T(8,128)S(1)}, f32[16,128,128]{2,1,0:T(8,128)S(1)}) custom-call(s32[832]{0:T(1024)S(1)} %broadcast_add_fusion.1.refs_0_.refs_3_, s32[416]{0:T(512)S(1)} %get-tuple-element.42.refs_1_.refs_4_, ...), custom_call_target="tpu_custom_call" | custom-call | flops 1610612736 | bytes 13631488 | tf_op jit(solution)/shard_map/tile_products/pallas_call | solution.py:160
  71.2 1.3 collective-permute-start.9
  72.6 12.0 %tile_products.5 = (bf16[16,128,128]{2,1,0:T(8,128)(2,1)S(1)}, bf16[16,128,128]{2,1,0:T(8,128)(2,1)S(1)}, bf16[16,128,128]{2,1,0:T(8,128)(2,1)S(1)}, f32[16,128,128]{2,1,0:T(8,128)S(1)}, f32[16,128,128]{2,1,0:T(8,128)S(1)}) custom-call(s32[832]{0:T(1024)S(1)} %broadcast_add_fusion.refs_0_, s32[416]{0:T(512)S(1)} %get-tuple-element.41.refs_1_, ...), custom_call_target="tpu_custom_call" | custom-call | flops 1610612736 | bytes 13631488 | tf_op jit(solution)/shard_map/tile_products/pallas_call | solution.py:160
  84.6 1.3 collective-permute-start.20
  85.9 1.3 collective-permute-start.7
  87.2 1.3 collective-permute-start.8
  88.7 5.2 %collective-permute-start.10 = (bf16[2048,128]{1,0:T(8,128)(2,1)S(1)}, bf16[2048,128]{1,0:T(8,128)(2,1)S(1)}, u32[]{:S(2)}, u32[]{:S(2)}) collective-permute-start(bf16[2048,128]{1,0:T(8,128)(2,1)S(1)} %fusion.8), channel_id=1, source_target_pairs={{0,2},{1,3},{3,1},{2,0},{4,6},{5,7},{7,5},{6,4},{8,10},{9,11},{11,... | collective-permute-start | bytes 1572872 | tf_op jit(solution)/shard_map/ppermute | solution.py:276
  93.9 4.0 %collective-permute-start.18 = (bf16[2048,128]{1,0:T(8,128)(2,1)S(1)}, bf16[2048,128]{1,0:T(8,128)(2,1)S(1)}, u32[]{:S(2)}, u32[]{:S(2)}) collective-permute-start(bf16[2048,128]{1,0:T(8,128)(2,1)S(1)} %bitcast.64), channel_id=1, source_target_pairs={{0,1},{1,2},{2,3},{4,5},{5,6},{6,7},{8,9},{9,10},{10,11},{12,13},{... | collective-permute-start | bytes 1572872 | tf_op jit(solution)/shard_map/ppermute | solution.py:276
  97.9 1.3 collective-permute-start.19
  99.3 8.9 %collective-permute-done.7 = bf16[2048,128]{1,0:T(8,128)(2,1)S(1)} collective-permute-done((bf16[2048,128]{1,0:T(8,128)(2,1)S(1)}, bf16[2048,128]{1,0:T(8,128)(2,1)S(1)}, u32[]{:S(2)}, u32[]{:S(2)}) %collective-permute-start.7) | collective-permute-done | bytes 524320 | tf_op jit(solution)/shard_map/ppermute | solution.py:276
  108.2 2.2 %collective-permute-start.21 = (bf16[2048,128]{1,0:T(8,128)(2,1)S(1)}, bf16[2048,128]{1,0:T(8,128)(2,1)S(1)}, u32[]{:S(2)}, u32[]{:S(2)}) collective-permute-start(bf16[2048,128]{1,0:T(8,128)(2,1)S(1)} %fusion.4), channel_id=1, source_target_pairs={{0,2},{1,3},{3,1},{2,0},{4,6},{5,7},{7,5},{6,4},{8,10},{9,11},{11,... | collective-permute-start | bytes 1572872 | tf_op jit(solution)/shard_map/ppermute | solution.py:276
  110.4 23.0 %collective-permute-done.10 = bf16[2048,128]{1,0:T(8,128)(2,1)S(1)} collective-permute-done((bf16[2048,128]{1,0:T(8,128)(2,1)S(1)}, bf16[2048,128]{1,0:T(8,128)(2,1)S(1)}, u32[]{:S(2)}, u32[]{:S(2)}) %collective-permute-start.10) | collective-permute-done | bytes 524320 | tf_op jit(solution)/shard_map/ppermute | solution.py:276
  134.2 26.5 %collective-permute-done.21 = bf16[2048,128]{1,0:T(8,128)(2,1)S(1)} collective-permute-done((bf16[2048,128]{1,0:T(8,128)(2,1)S(1)}, bf16[2048,128]{1,0:T(8,128)(2,1)S(1)}, u32[]{:S(2)}, u32[]{:S(2)}) %collective-permute-start.21) | collective-permute-done | bytes 524320 | tf_op jit(solution)/shard_map/ppermute | solution.py:276
  160.9 1.4 fusion.1
  (57 shorter events, 8.8 us)
Async XLA Ops:
  1.3 16.8 %collective-permute-start.16 = (bf16[2048,128]{1,0:T(8,128)(2,1)S(1)}, bf16[2048,128]{1,0:T(8,128)(2,1)S(1)}, u32[]{:S(2)}, u32[]{:S(2)}) collective-permute-start(bf16[2048,128]{1,0:T(8,128)(2,1)S(1)} %get-tuple-element.37), channel_id=1, source_target_pairs={{0,24},{4,28},{8,16},{12,20},{16,8},{20,12},{24,0},{28,4},{1,25},{... | collective-permute-start | bytes 1572872 | tf_op jit(solution)/shard_map/ppermute | solution.py:192
  5.3 24.1 %collective-permute-start.14 = (bf16[2048,128]{1,0:T(8,128)(2,1)S(1)}, bf16[2048,128]{1,0:T(8,128)(2,1)S(1)}, u32[]{:S(2)}, u32[]{:S(2)}) collective-permute-start(bf16[2048,128]{1,0:T(8,128)(2,1)S(1)} %get-tuple-element.37), channel_id=1, source_target_pairs={{0,16},{4,20},{8,24},{12,28},{16,0},{20,4},{24,8},{28,12},{1,17},{... | collective-permute-start | bytes 1572872 | tf_op jit(solution)/shard_map/ppermute | solution.py:192
  5.8 45.2 %collective-permute-start.5 = (bf16[2048,128]{1,0:T(8,128)(2,1)S(1)}, bf16[2048,128]{1,0:T(8,128)(2,1)}, u32[]{:S(2)}, u32[]{:S(2)}) collective-permute-start(bf16[2048,128]{1,0:T(8,128)(2,1)S(1)} %get-tuple-element.38), channel_id=1, source_target_pairs={{0,16},{4,20},{8,24},{12,28},{16,0},{20,4},{24,8},{28,12},{1,17},{... | collective-permute-start | bytes 1572872 | tf_op jit(solution)/shard_map/ppermute | solution.py:192
  7.3 43.7 %collective-permute-start.3 = (bf16[2048,128]{1,0:T(8,128)(2,1)S(1)}, bf16[2048,128]{1,0:T(8,128)(2,1)}, u32[]{:S(2)}, u32[]{:S(2)}) collective-permute-start(bf16[2048,128]{1,0:T(8,128)(2,1)S(1)} %get-tuple-element.38), channel_id=1, source_target_pairs={{0,8},{4,12},{8,0},{12,4},{16,24},{20,28},{24,16},{28,20},{1,9},{5... | collective-permute-start | bytes 1572872 | tf_op jit(solution)/shard_map/ppermute | solution.py:192
  7.8 43.7 %collective-permute-start = (bf16[2048,128]{1,0:T(8,128)(2,1)S(1)}, bf16[2048,128]{1,0:T(8,128)(2,1)S(1)}, u32[]{:S(2)}, u32[]{:S(2)}) collective-permute-start(bf16[2048,128]{1,0:T(8,128)(2,1)S(1)} %get-tuple-element.38), channel_id=1, source_target_pairs={{0,24},{4,28},{8,16},{12,20},{16,8},{20,12},{24,0},{28,4},{1,25},{... | collective-permute-start | bytes 1572872 | tf_op jit(solution)/shard_map/ppermute | solution.py:192
  18.1 35.0 %collective-permute-start.12 = (bf16[2048,128]{1,0:T(8,128)(2,1)S(1)}, bf16[2048,128]{1,0:T(8,128)(2,1)S(1)}, u32[]{:S(2)}, u32[]{:S(2)}) collective-permute-start(bf16[2048,128]{1,0:T(8,128)(2,1)S(1)} %get-tuple-element.37), channel_id=1, source_target_pairs={{0,8},{4,12},{8,0},{12,4},{16,24},{20,28},{24,16},{28,20},{1,9},{5... | collective-permute-start | bytes 1572872 | tf_op jit(solution)/shard_map/ppermute | solution.py:192
  29.4 24.2 %collective-permute-start.2 = (bf16[2048,128]{1,0:T(8,128)(2,1)S(1)}, bf16[2048,128]{1,0:T(8,128)(2,1)}, u32[]{:S(2)}, u32[]{:S(2)}) collective-permute-start(bf16[2048,128]{1,0:T(8,128)(2,1)S(1)} %get-tuple-element.38), channel_id=1, source_target_pairs={{0,4},{4,0},{8,12},{12,8},{16,20},{20,16},{24,28},{28,24},{1,5},{5... | collective-permute-start | bytes 1572872 | tf_op jit(solution)/shard_map/ppermute | solution.py:192
  51.0 2.7 %collective-permute-start.6 = (bf16[2048,128]{1,0:T(8,128)(2,1)}, bf16[2048,128]{1,0:T(8,128)(2,1)}, u32[]{:S(2)}, u32[]{:S(2)}) collective-permute-start(bf16[2048,128]{1,0:T(8,128)(2,1)} %collective-permute-done.5), channel_id=1, source_target_pairs={{0,4},{4,0},{8,12},{12,8},{16,20},{20,16},{24,28},{28,24},{1,5},{5... | collective-permute-start | bytes 1572872 | tf_op jit(solution)/shard_map/ppermute | solution.py:192
  51.0 3.1 %collective-permute-start.4 = (bf16[2048,128]{1,0:T(8,128)(2,1)}, bf16[2048,128]{1,0:T(8,128)(2,1)}, u32[]{:S(2)}, u32[]{:S(2)}) collective-permute-start(bf16[2048,128]{1,0:T(8,128)(2,1)} %collective-permute-done.3), channel_id=1, source_target_pairs={{0,4},{4,0},{8,12},{12,8},{16,20},{20,16},{24,28},{28,24},{1,5},{5... | collective-permute-start | bytes 1572872 | tf_op jit(solution)/shard_map/ppermute | solution.py:192
  51.5 13.8 %collective-permute-start.1 = (bf16[2048,128]{1,0:T(8,128)(2,1)S(1)}, bf16[2048,128]{1,0:T(8,128)(2,1)}, u32[]{:S(2)}, u32[]{:S(2)}) collective-permute-start(bf16[2048,128]{1,0:T(8,128)(2,1)S(1)} %collective-permute-done), channel_id=1, source_target_pairs={{0,4},{4,0},{8,12},{12,8},{16,20},{20,16},{24,28},{28,24},{1,5},{5... | collective-permute-start | bytes 1572872 | tf_op jit(solution)/shard_map/ppermute | solution.py:192
  53.1 19.5 %collective-permute-start.11 = (bf16[2048,128]{1,0:T(8,128)(2,1)S(1)}, bf16[2048,128]{1,0:T(8,128)(2,1)S(1)}, u32[]{:S(2)}, u32[]{:S(2)}) collective-permute-start(bf16[2048,128]{1,0:T(8,128)(2,1)S(1)} %get-tuple-element.37), channel_id=1, source_target_pairs={{0,4},{4,0},{8,12},{12,8},{16,20},{20,16},{24,28},{28,24},{1,5},{5... | collective-permute-start | bytes 1572872 | tf_op jit(solution)/shard_map/ppermute | solution.py:192
  53.6 19.0 %collective-permute-start.17 = (bf16[2048,128]{1,0:T(8,128)(2,1)S(1)}, bf16[2048,128]{1,0:T(8,128)(2,1)S(1)}, u32[]{:S(2)}, u32[]{:S(2)}) collective-permute-start(bf16[2048,128]{1,0:T(8,128)(2,1)S(1)} %collective-permute-done.16), channel_id=1, source_target_pairs={{0,4},{4,0},{8,12},{12,8},{16,20},{20,16},{24,28},{28,24},{1,5},{5... | collective-permute-start | bytes 1572872 | tf_op jit(solution)/shard_map/ppermute | solution.py:192
  53.7 18.9 %collective-permute-start.15 = (bf16[2048,128]{1,0:T(8,128)(2,1)S(1)}, bf16[2048,128]{1,0:T(8,128)(2,1)S(1)}, u32[]{:S(2)}, u32[]{:S(2)}) collective-permute-start(bf16[2048,128]{1,0:T(8,128)(2,1)S(1)} %collective-permute-done.14), channel_id=1, source_target_pairs={{0,4},{4,0},{8,12},{12,8},{16,20},{20,16},{24,28},{28,24},{1,5},{5... | collective-permute-start | bytes 1572872 | tf_op jit(solution)/shard_map/ppermute | solution.py:192
  54.1 18.5 %collective-permute-start.13 = (bf16[2048,128]{1,0:T(8,128)(2,1)S(1)}, bf16[2048,128]{1,0:T(8,128)(2,1)S(1)}, u32[]{:S(2)}, u32[]{:S(2)}) collective-permute-start(bf16[2048,128]{1,0:T(8,128)(2,1)S(1)} %collective-permute-done.12), channel_id=1, source_target_pairs={{0,4},{4,0},{8,12},{12,8},{16,20},{20,16},{24,28},{28,24},{1,5},{5... | collective-permute-start | bytes 1572872 | tf_op jit(solution)/shard_map/ppermute | solution.py:192
  71.2 17.3 %collective-permute-start.9 = (bf16[2048,128]{1,0:T(8,128)(2,1)S(1)}, bf16[2048,128]{1,0:T(8,128)(2,1)S(1)}, u32[]{:S(2)}, u32[]{:S(2)}) collective-permute-start(bf16[2048,128]{1,0:T(8,128)(2,1)S(1)} %bitcast.65), channel_id=1, source_target_pairs={{0,1},{3,2},{4,5},{7,6},{8,9},{11,10},{12,13},{15,14},{16,17},{19,... | collective-permute-start | bytes 1572872 | tf_op jit(solution)/shard_map/ppermute | solution.py:276
  84.6 13.3 %collective-permute-start.20 = (bf16[2048,128]{1,0:T(8,128)(2,1)S(1)}, bf16[2048,128]{1,0:T(8,128)(2,1)S(1)}, u32[]{:S(2)}, u32[]{:S(2)}) collective-permute-start(bf16[2048,128]{1,0:T(8,128)(2,1)S(1)} %bitcast.66), channel_id=1, source_target_pairs={{0,1},{3,2},{4,5},{7,6},{8,9},{11,10},{12,13},{15,14},{16,17},{19,... | collective-permute-start | bytes 1572872 | tf_op jit(solution)/shard_map/ppermute | solution.py:276
  85.9 22.3 %collective-permute-start.7 = (bf16[2048,128]{1,0:T(8,128)(2,1)S(1)}, bf16[2048,128]{1,0:T(8,128)(2,1)S(1)}, u32[]{:S(2)}, u32[]{:S(2)}) collective-permute-start(bf16[2048,128]{1,0:T(8,128)(2,1)S(1)} %bitcast.63), channel_id=1, source_target_pairs={{0,1},{1,2},{2,3},{4,5},{5,6},{6,7},{8,9},{9,10},{10,11},{12,13},{... | collective-permute-start | bytes 1572872 | tf_op jit(solution)/shard_map/ppermute | solution.py:276
  87.2 23.2 %collective-permute-start.8 = (bf16[2048,128]{1,0:T(8,128)(2,1)S(1)}, bf16[2048,128]{1,0:T(8,128)(2,1)S(1)}, u32[]{:S(2)}, u32[]{:S(2)}) collective-permute-start(bf16[2048,128]{1,0:T(8,128)(2,1)S(1)} %bitcast.61), channel_id=1, source_target_pairs={{1,0},{2,1},{3,2},{5,4},{6,5},{7,6},{9,8},{10,9},{11,10},{13,12},{... | collective-permute-start | bytes 1572872 | tf_op jit(solution)/shard_map/ppermute | solution.py:276
  88.7 44.8 %collective-permute-start.10 = (bf16[2048,128]{1,0:T(8,128)(2,1)S(1)}, bf16[2048,128]{1,0:T(8,128)(2,1)S(1)}, u32[]{:S(2)}, u32[]{:S(2)}) collective-permute-start(bf16[2048,128]{1,0:T(8,128)(2,1)S(1)} %fusion.8), channel_id=1, source_target_pairs={{0,2},{1,3},{3,1},{2,0},{4,6},{5,7},{7,5},{6,4},{8,10},{9,11},{11,... | collective-permute-start | bytes 1572872 | tf_op jit(solution)/shard_map/ppermute | solution.py:276
  93.9 40.3 %collective-permute-start.18 = (bf16[2048,128]{1,0:T(8,128)(2,1)S(1)}, bf16[2048,128]{1,0:T(8,128)(2,1)S(1)}, u32[]{:S(2)}, u32[]{:S(2)}) collective-permute-start(bf16[2048,128]{1,0:T(8,128)(2,1)S(1)} %bitcast.64), channel_id=1, source_target_pairs={{0,1},{1,2},{2,3},{4,5},{5,6},{6,7},{8,9},{9,10},{10,11},{12,13},{... | collective-permute-start | bytes 1572872 | tf_op jit(solution)/shard_map/ppermute | solution.py:276
  97.9 36.3 %collective-permute-start.19 = (bf16[2048,128]{1,0:T(8,128)(2,1)S(1)}, bf16[2048,128]{1,0:T(8,128)(2,1)S(1)}, u32[]{:S(2)}, u32[]{:S(2)}) collective-permute-start(bf16[2048,128]{1,0:T(8,128)(2,1)S(1)} %bitcast.62), channel_id=1, source_target_pairs={{1,0},{2,1},{3,2},{5,4},{6,5},{7,6},{9,8},{10,9},{11,10},{13,12},{... | collective-permute-start | bytes 1572872 | tf_op jit(solution)/shard_map/ppermute | solution.py:276
  99.2 34.6 %copy-start = (bf16[256,256]{1,0:T(8,128)(2,1)S(1)}, bf16[256,256]{1,0:T(8,128)(2,1)}, u32[]{:S(2)}) copy-start(bf16[256,256]{1,0:T(8,128)(2,1)} %param.12) | copy-start | bytes 393220
  99.2 34.6 %copy-start.1 = (f32[256]{0:T(256)S(1)}, f32[256]{0:T(256)}, u32[]{:S(2)}) copy-start(f32[256]{0:T(256)} %param.13) | copy-start | bytes 3076
  108.2 52.4 %collective-permute-start.21 = (bf16[2048,128]{1,0:T(8,128)(2,1)S(1)}, bf16[2048,128]{1,0:T(8,128)(2,1)S(1)}, u32[]{:S(2)}, u32[]{:S(2)}) collective-permute-start(bf16[2048,128]{1,0:T(8,128)(2,1)S(1)} %fusion.4), channel_id=1, source_target_pairs={{0,2},{1,3},{3,1},{2,0},{4,6},{5,7},{7,5},{6,4},{8,10},{9,11},{11,... | collective-permute-start | bytes 1572872 | tf_op jit(solution)/shard_map/ppermute | solution.py:276

commit v2 on v1

--- a/solution.py
+++ b/solution.py
@@ -42,8 +42,9 @@
     group_ids = jnp.arange(room // GROUP, dtype=jnp.int32)
     group_rows = jnp.sum((ends[None, :] <= group_ids[:, None]).astype(jnp.int32), axis=1)
     group_rows = jnp.minimum(group_rows, row_tiles - 1)
-    turns = (total + (UNROLL - 1)) // UNROLL
-    return entries, group_rows, turns.reshape(1)
+    closing = ends.reshape(lax.axis_size("col"), -1)[:, -1]
+    last_turns = jnp.maximum((closing + (UNROLL - 1)) // UNROLL, 1) - 1
+    return entries, group_rows, last_turns
 
 
 def tile_kernel(*refs, lists, parts, begun, keep, col_bits, narrow, wide):
@@ -54,7 +55,7 @@
     tiles = refs[len(parts)]
     started = refs[len(parts) + 1] if begun else None
     outs = refs[len(parts) + 1 + begun :][: narrow + wide + keep]
-    sums, panel, ring, tile_sems, whole_sem, *earlier = refs[len(parts) + 1 + begun + narrow + wide + keep :]
+    sums, panel, ring, tile_sems, whole_sem, save_sems, *earlier = refs[len(parts) + 1 + begun + narrow + wide + keep :]
     block_tiles = blocks[0].shape[0]
     zero_seat = STAGES * BATCH
     spare = place[parts[0]] * block_tiles
@@ -67,6 +68,10 @@
 
     def first_fetches(entries, count):
         lax.fori_loop(0, jnp.minimum(count, STAGES - 1), lambda turn, carry: fetch(entries, turn) or carry, 0)
+
+    def save(number):
+        piece = pl.ds(number * block_tiles, block_tiles)
+        return pltpu.make_async_copy(sums.at[piece], outs[0].at[piece], save_sems.at[number])
 
     def step(ahead, entries, group_rows, turn, carry):
         stage = lax.rem(turn, STAGES)
@@ -93,9 +98,12 @@
             )
         for group in range(UNROLL):
             sums[group_rows[turn * UNROLL + group]] += products[group]
+        if keep:
+            for number in range(plans[0][2].shape[0]):
+                pl.when(turn == plans[0][2][number])(save(number).start)
         return carry
 
-    first_fetches(plans[0][0], plans[0][2][0])
+    first_fetches(plans[0][0], plans[0][2][plans[0][2].shape[0] - 1] + 1)
     ring[zero_seat] = jnp.zeros(ring.shape[1:], ring.dtype)
     if begun:
         restore = pltpu.make_async_copy(started.at[pl.ds(0, sums.shape[0])], earlier[0], whole_sem)
@@ -104,7 +112,7 @@
     for number, part in enumerate(parts):
         panel[pl.ds(place[part] * block_tiles, block_tiles)] = blocks[number][...]
     for number, (entries, group_rows, turns) in enumerate(plans):
-        count = turns[0]
+        count = turns[turns.shape[0] - 1] + 1
         if number:
             first_fetches(entries, count)
         steady = jnp.maximum(count - (STAGES - 1), 0)
@@ -112,9 +120,8 @@
         lax.fori_loop(steady, count, functools.partial(step, 0, entries, group_rows), 0)
 
     if keep:
-        save = pltpu.make_async_copy(sums, outs[0].at[pl.ds(0, sums.shape[0])], whole_sem)
-        save.start()
-        save.wait()
+        for number in range(plans[0][2].shape[0]):
+            save(number).wait()
         return
     if begun:
         restore.wait()
@@ -156,6 +163,7 @@
         pltpu.VMEM((STAGES * BATCH + 1, tile_size, tile_size), jnp.bfloat16),
         pltpu.SemaphoreType.DMA((STAGES,)),
         pltpu.SemaphoreType.DMA(()),
+        pltpu.SemaphoreType.DMA((row_tiles // block_tiles,)),
     ] + [sums] * (begun is not None)
     outs = pl.pallas_call(
         functools.partial(

time: 165 us -> 163 us (0.988)
  waiting for transfers between devices: 92.6 us -> 96.9 us
  starting transfers between devices: 29.6 us -> 27.2 us
  Pallas kernels: 29 us -> 27.2 us
    ppermute x8, waiting for transfers between devices: 58.4 us -> 60.8 us  [move(): lax.ppermute(value, 'col', pairs)]
    ppermute x8, starting transfers between devices: 18 us -> 15.8 us  [move(): lax.ppermute(value, 'col', pairs)]
    ppermute x14, waiting for transfers between devices: 34.2 us -> 36.1 us  [swap(): return lax.ppermute(value, 'row', [(i, i ^ bits) for i in range(size)])]
    pallas_call x3, Pallas kernels: 29 us -> 27.2 us  [tile_products(): pl.pallas_call(functools.partial(tile_kernel, lists=len(plans), parts=par...]
  transfers between devices with their start and end apart: 22 -> 22, of which waited for: 6 -> 8; matrix products, arithmetic and copies ran while one was open for 4% -> 4% of each run, Pallas kernels for 18% -> 17%
where the time goes in v2:
time: 163 us; the launch traced here: 160 us
  waiting for transfers between devices  96.9 us (59%)
  starting transfers between devices  27.2 us (17%)
  Pallas kernels  27.2 us (17%)
  other arithmetic  5.4 us (3%)
  matrix products  1.8 us (1%)
    ppermute x8, waiting for transfers between devices, move(): lax.ppermute(value, 'col', pairs)  60.8 us
    ppermute x14, waiting for transfers between devices, swap(): return lax.ppermute(value, 'row', [(i, i ^ bits) for i in range(size)])  36.1 us
    pallas_call x3, Pallas kernels, tile_products(): pl.pallas_call(functools.partial(tile_kernel, lists=len(plans), parts=par...  27.2 us
    ppermute x8, starting transfers between devices, move(): lax.ppermute(value, 'col', pairs)  15.8 us
    ppermute x14, starting transfers between devices, swap(): return lax.ppermute(value, 'row', [(i, i ^ bits) for i in range(size)])  11.4 us
  transfers between devices with their start and end apart: 22, of which 8 were waited for; matrix products, arithmetic and copies ran while one was open for 4% of the time, Pallas kernels for 17%

profile of v2, /device:TPU:0, one launch (start us, length us, event | category | flops | bytes accessed | tf_op | source)
XLA Modules:
  0.0 160.2 jit_solution(6593571103705306115)
XLA Ops:
  0.0 1.3 fusion.23
  1.3 4.0 %collective-permute-start.16 = (bf16[2048,128]{1,0:T(8,128)(2,1)S(1)}, bf16[2048,128]{1,0:T(8,128)(2,1)S(1)}, u32[]{:S(2)}, u32[]{:S(2)}) collective-permute-start(bf16[2048,128]{1,0:T(8,128)(2,1)S(1)} %get-tuple-element.33), channel_id=1, source_target_pairs={{0,24},{4,28},{8,16},{12,20},{16,8},{20,12},{24,0},{28,4},{1,25},{... | collective-permute-start | bytes 1572872 | tf_op jit(solution)/shard_map/ppermute | solution.py:200
  5.8 1.5 collective-permute-start.5
  7.8 1.4 collective-permute-start
  9.3 0.7 compare_reduce_fusion
  10.7 0.7 reduce.1
  14.1 4.0 %collective-permute-done.16 = bf16[2048,128]{1,0:T(8,128)(2,1)S(1)} collective-permute-done((bf16[2048,128]{1,0:T(8,128)(2,1)S(1)}, bf16[2048,128]{1,0:T(8,128)(2,1)S(1)}, u32[]{:S(2)}, u32[]{:S(2)}) %collective-permute-start.16) | collective-permute-done | bytes 524320 | tf_op jit(solution)/shard_map/ppermute | solution.py:200
  18.1 2.0 %collective-permute-start.12 = (bf16[2048,128]{1,0:T(8,128)(2,1)S(1)}, bf16[2048,128]{1,0:T(8,128)(2,1)S(1)}, u32[]{:S(2)}, u32[]{:S(2)}) collective-permute-start(bf16[2048,128]{1,0:T(8,128)(2,1)S(1)} %get-tuple-element.33), channel_id=1, source_target_pairs={{0,8},{4,12},{8,0},{12,4},{16,24},{20,28},{24,16},{28,20},{1,9},{5... | collective-permute-start | bytes 1572872 | tf_op jit(solution)/shard_map/ppermute | solution.py:200
  20.0 9.3 %collective-permute-done.14 = bf16[2048,128]{1,0:T(8,128)(2,1)S(1)} collective-permute-done((bf16[2048,128]{1,0:T(8,128)(2,1)S(1)}, bf16[2048,128]{1,0:T(8,128)(2,1)S(1)}, u32[]{:S(2)}, u32[]{:S(2)}) %collective-permute-start.14) | collective-permute-done | bytes 524320 | tf_op jit(solution)/shard_map/ppermute | solution.py:200
  29.4 21.5 %collective-permute-done.5 = bf16[2048,128]{1,0:T(8,128)(2,1)S(1)} collective-permute-done((bf16[2048,128]{1,0:T(8,128)(2,1)S(1)}, bf16[2048,128]{1,0:T(8,128)(2,1)S(1)}, u32[]{:S(2)}, u32[]{:S(2)}) %collective-permute-start.5) | collective-permute-done | bytes 524320 | tf_op jit(solution)/shard_map/ppermute | solution.py:200
  53.7 9.6 %tile_products.3.refs_8_ = f32[384,128,128]{2,1,0:T(8,128)} custom-call(s32[832]{0:T(1024)S(1)} %broadcast_add_fusion.refs_0_, s32[416]{0:T(512)S(1)} %get-tuple-element.37.refs_1_, s32[4]{0:T(128)S(1)} %get-tuple-element.39.refs_2_, s32[8]{0:T(128)S(1)} %iota_xor_fusion.refs_3_.refs_6_, s32[5]{0:T(128)S(1)} %compare_select_fusion.4.refs_4_.refs_7_, ...), custom_call_target="tpu_custom_call" | custom-call | flops 1610612736 | bytes 13631488 | tf_op jit(solution)/shard_map/tile_products/pallas_call | solution.py:168
  63.3 5.5 %tile_products.4 = (bf16[16,128,128]{2,1,0:T(8,128)(2,1)S(1)}, bf16[16,128,128]{2,1,0:T(8,128)(2,1)S(1)}, bf16[16,128,128]{2,1,0:T(8,128)(2,1)S(1)}, f32[16,128,128]{2,1,0:T(8,128)S(1)}, f32[16,128,128]{2,1,0:T(8,128)S(1)}) custom-call(s32[832]{0:T(1024)S(1)} %broadcast_add_fusion.1.refs_0_.refs_3_, s32[416]{0:T(512)S(1)} %get-tuple-element.38.refs_1_.refs_4_, ...), custom_call_target="tpu_custom_call" | custom-call | flops 1610612736 | bytes 13631488 | tf_op jit(solution)/shard_map/tile_products/pallas_call | solution.py:168
  68.9 1.3 collective-permute-start.9
  70.2 12.0 %tile_products.5 = (bf16[16,128,128]{2,1,0:T(8,128)(2,1)S(1)}, bf16[16,128,128]{2,1,0:T(8,128)(2,1)S(1)}, bf16[16,128,128]{2,1,0:T(8,128)(2,1)S(1)}, f32[16,128,128]{2,1,0:T(8,128)S(1)}, f32[16,128,128]{2,1,0:T(8,128)S(1)}) custom-call(s32[832]{0:T(1024)S(1)} %broadcast_add_fusion.refs_0_, s32[416]{0:T(512)S(1)} %get-tuple-element.37.refs_1_, ...), custom_call_target="tpu_custom_call" | custom-call | flops 1610612736 | bytes 13631488 | tf_op jit(solution)/shard_map/tile_products/pallas_call | solution.py:168
  82.3 1.3 collective-permute-start.20
  83.6 1.3 collective-permute-start.7
  84.9 1.3 collective-permute-start.8
  86.3 5.3 %collective-permute-start.10 = (bf16[2048,128]{1,0:T(8,128)(2,1)S(1)}, bf16[2048,128]{1,0:T(8,128)(2,1)S(1)}, u32[]{:S(2)}, u32[]{:S(2)}) collective-permute-start(bf16[2048,128]{1,0:T(8,128)(2,1)S(1)} %fusion.8), channel_id=1, source_target_pairs={{0,2},{1,3},{3,1},{2,0},{4,6},{5,7},{7,5},{6,4},{8,10},{9,11},{11,... | collective-permute-start | bytes 1572872 | tf_op jit(solution)/shard_map/ppermute | solution.py:284
  91.7 4.0 %collective-permute-start.18 = (bf16[2048,128]{1,0:T(8,128)(2,1)S(1)}, bf16[2048,128]{1,0:T(8,128)(2,1)S(1)}, u32[]{:S(2)}, u32[]{:S(2)}) collective-permute-start(bf16[2048,128]{1,0:T(8,128)(2,1)S(1)} %bitcast.67), channel_id=1, source_target_pairs={{0,1},{1,2},{2,3},{4,5},{5,6},{6,7},{8,9},{9,10},{10,11},{12,13},{... | collective-permute-start | bytes 1572872 | tf_op jit(solution)/shard_map/ppermute | solution.py:284
  95.7 1.3 collective-permute-start.19
  97.1 8.6 %collective-permute-done.7 = bf16[2048,128]{1,0:T(8,128)(2,1)S(1)} collective-permute-done((bf16[2048,128]{1,0:T(8,128)(2,1)S(1)}, bf16[2048,128]{1,0:T(8,128)(2,1)S(1)}, u32[]{:S(2)}, u32[]{:S(2)}) %collective-permute-start.7) | collective-permute-done | bytes 524320 | tf_op jit(solution)/shard_map/ppermute | solution.py:284
  105.7 24.2 %collective-permute-done.10 = bf16[2048,128]{1,0:T(8,128)(2,1)S(1)} collective-permute-done((bf16[2048,128]{1,0:T(8,128)(2,1)S(1)}, bf16[2048,128]{1,0:T(8,128)(2,1)S(1)}, u32[]{:S(2)}, u32[]{:S(2)}) %collective-permute-start.10) | collective-permute-done | bytes 524320 | tf_op jit(solution)/shard_map/ppermute | solution.py:284
  130.6 28.0 %collective-permute-done.21 = bf16[2048,128]{1,0:T(8,128)(2,1)S(1)} collective-permute-done((bf16[2048,128]{1,0:T(8,128)(2,1)S(1)}, bf16[2048,128]{1,0:T(8,128)(2,1)S(1)}, u32[]{:S(2)}, u32[]{:S(2)}) %collective-permute-start.21) | collective-permute-done | bytes 524320 | tf_op jit(solution)/shard_map/ppermute | solution.py:284
  158.9 1.4 fusion.1
  (62 shorter events, 8.3 us)
Async XLA Ops:
  1.3 16.8 %collective-permute-start.16 = (bf16[2048,128]{1,0:T(8,128)(2,1)S(1)}, bf16[2048,128]{1,0:T(8,128)(2,1)S(1)}, u32[]{:S(2)}, u32[]{:S(2)}) collective-permute-start(bf16[2048,128]{1,0:T(8,128)(2,1)S(1)} %get-tuple-element.33), channel_id=1, source_target_pairs={{0,24},{4,28},{8,16},{12,20},{16,8},{20,12},{24,0},{28,4},{1,25},{... | collective-permute-start | bytes 1572872 | tf_op jit(solution)/shard_map/ppermute | solution.py:200
  5.3 24.1 %collective-permute-start.14 = (bf16[2048,128]{1,0:T(8,128)(2,1)S(1)}, bf16[2048,128]{1,0:T(8,128)(2,1)S(1)}, u32[]{:S(2)}, u32[]{:S(2)}) collective-permute-start(bf16[2048,128]{1,0:T(8,128)(2,1)S(1)} %get-tuple-element.33), channel_id=1, source_target_pairs={{0,16},{4,20},{8,24},{12,28},{16,0},{20,4},{24,8},{28,12},{1,17},{... | collective-permute-start | bytes 1572872 | tf_op jit(solution)/shard_map/ppermute | solution.py:200
  5.8 45.1 %collective-permute-start.5 = (bf16[2048,128]{1,0:T(8,128)(2,1)S(1)}, bf16[2048,128]{1,0:T(8,128)(2,1)S(1)}, u32[]{:S(2)}, u32[]{:S(2)}) collective-permute-start(bf16[2048,128]{1,0:T(8,128)(2,1)S(1)} %get-tuple-element.34), channel_id=1, source_target_pairs={{0,16},{4,20},{8,24},{12,28},{16,0},{20,4},{24,8},{28,12},{1,17},{... | collective-permute-start | bytes 1572872 | tf_op jit(solution)/shard_map/ppermute | solution.py:200
  7.3 43.6 %collective-permute-start.3 = (bf16[2048,128]{1,0:T(8,128)(2,1)S(1)}, bf16[2048,128]{1,0:T(8,128)(2,1)}, u32[]{:S(2)}, u32[]{:S(2)}) collective-permute-start(bf16[2048,128]{1,0:T(8,128)(2,1)S(1)} %get-tuple-element.34), channel_id=1, source_target_pairs={{0,8},{4,12},{8,0},{12,4},{16,24},{20,28},{24,16},{28,20},{1,9},{5... | collective-permute-start | bytes 1572872 | tf_op jit(solution)/shard_map/ppermute | solution.py:200
  7.8 43.6 %collective-permute-start = (bf16[2048,128]{1,0:T(8,128)(2,1)S(1)}, bf16[2048,128]{1,0:T(8,128)(2,1)S(1)}, u32[]{:S(2)}, u32[]{:S(2)}) collective-permute-start(bf16[2048,128]{1,0:T(8,128)(2,1)S(1)} %get-tuple-element.34), channel_id=1, source_target_pairs={{0,24},{4,28},{8,16},{12,20},{16,8},{20,12},{24,0},{28,4},{1,25},{... | collective-permute-start | bytes 1572872 | tf_op jit(solution)/shard_map/ppermute | solution.py:200
  18.1 33.5 %collective-permute-start.12 = (bf16[2048,128]{1,0:T(8,128)(2,1)S(1)}, bf16[2048,128]{1,0:T(8,128)(2,1)S(1)}, u32[]{:S(2)}, u32[]{:S(2)}) collective-permute-start(bf16[2048,128]{1,0:T(8,128)(2,1)S(1)} %get-tuple-element.33), channel_id=1, source_target_pairs={{0,8},{4,12},{8,0},{12,4},{16,24},{20,28},{24,16},{28,20},{1,9},{5... | collective-permute-start | bytes 1572872 | tf_op jit(solution)/shard_map/ppermute | solution.py:200
  29.4 22.7 %collective-permute-start.2 = (bf16[2048,128]{1,0:T(8,128)(2,1)S(1)}, bf16[2048,128]{1,0:T(8,128)(2,1)S(1)}, u32[]{:S(2)}, u32[]{:S(2)}) collective-permute-start(bf16[2048,128]{1,0:T(8,128)(2,1)S(1)} %get-tuple-element.34), channel_id=1, source_target_pairs={{0,4},{4,0},{8,12},{12,8},{16,20},{20,16},{24,28},{28,24},{1,5},{5... | collective-permute-start | bytes 1572872 | tf_op jit(solution)/shard_map/ppermute | solution.py:200
  50.9 1.9 %collective-permute-start.6 = (bf16[2048,128]{1,0:T(8,128)(2,1)S(1)}, bf16[2048,128]{1,0:T(8,128)(2,1)S(1)}, u32[]{:S(2)}, u32[]{:S(2)}) collective-permute-start(bf16[2048,128]{1,0:T(8,128)(2,1)S(1)} %collective-permute-done.5), channel_id=1, source_target_pairs={{0,4},{4,0},{8,12},{12,8},{16,20},{20,16},{24,28},{28,24},{1,5},{5... | collective-permute-start | bytes 1572872 | tf_op jit(solution)/shard_map/ppermute | solution.py:200
  50.9 2.6 %collective-permute-start.4 = (bf16[2048,128]{1,0:T(8,128)(2,1)}, bf16[2048,128]{1,0:T(8,128)(2,1)S(1)}, u32[]{:S(2)}, u32[]{:S(2)}) collective-permute-start(bf16[2048,128]{1,0:T(8,128)(2,1)} %collective-permute-done.3), channel_id=1, source_target_pairs={{0,4},{4,0},{8,12},{12,8},{16,20},{20,16},{24,28},{28,24},{1,5},{5... | collective-permute-start | bytes 1572872 | tf_op jit(solution)/shard_map/ppermute | solution.py:200
  51.4 11.9 %collective-permute-start.1 = (bf16[2048,128]{1,0:T(8,128)(2,1)S(1)}, bf16[2048,128]{1,0:T(8,128)(2,1)S(1)}, u32[]{:S(2)}, u32[]{:S(2)}) collective-permute-start(bf16[2048,128]{1,0:T(8,128)(2,1)S(1)} %collective-permute-done), channel_id=1, source_target_pairs={{0,4},{4,0},{8,12},{12,8},{16,20},{20,16},{24,28},{28,24},{1,5},{5... | collective-permute-start | bytes 1572872 | tf_op jit(solution)/shard_map/ppermute | solution.py:200
  51.6 18.6 %collective-permute-start.11 = (bf16[2048,128]{1,0:T(8,128)(2,1)S(1)}, bf16[2048,128]{1,0:T(8,128)(2,1)S(1)}, u32[]{:S(2)}, u32[]{:S(2)}) collective-permute-start(bf16[2048,128]{1,0:T(8,128)(2,1)S(1)} %get-tuple-element.33), channel_id=1, source_target_pairs={{0,4},{4,0},{8,12},{12,8},{16,20},{20,16},{24,28},{28,24},{1,5},{5... | collective-permute-start | bytes 1572872 | tf_op jit(solution)/shard_map/ppermute | solution.py:200
  52.1 18.1 %collective-permute-start.17 = (bf16[2048,128]{1,0:T(8,128)(2,1)S(1)}, bf16[2048,128]{1,0:T(8,128)(2,1)S(1)}, u32[]{:S(2)}, u32[]{:S(2)}) collective-permute-start(bf16[2048,128]{1,0:T(8,128)(2,1)S(1)} %collective-permute-done.16), channel_id=1, source_target_pairs={{0,4},{4,0},{8,12},{12,8},{16,20},{20,16},{24,28},{28,24},{1,5},{5... | collective-permute-start | bytes 1572872 | tf_op jit(solution)/shard_map/ppermute | solution.py:200
  52.8 17.4 %collective-permute-start.15 = (bf16[2048,128]{1,0:T(8,128)(2,1)S(1)}, bf16[2048,128]{1,0:T(8,128)(2,1)S(1)}, u32[]{:S(2)}, u32[]{:S(2)}) collective-permute-start(bf16[2048,128]{1,0:T(8,128)(2,1)S(1)} %collective-permute-done.14), channel_id=1, source_target_pairs={{0,4},{4,0},{8,12},{12,8},{16,20},{20,16},{24,28},{28,24},{1,5},{5... | collective-permute-start | bytes 1572872 | tf_op jit(solution)/shard_map/ppermute | solution.py:200
  53.6 16.7 %collective-permute-start.13 = (bf16[2048,128]{1,0:T(8,128)(2,1)S(1)}, bf16[2048,128]{1,0:T(8,128)(2,1)S(1)}, u32[]{:S(2)}, u32[]{:S(2)}) collective-permute-start(bf16[2048,128]{1,0:T(8,128)(2,1)S(1)} %collective-permute-done.12), channel_id=1, source_target_pairs={{0,4},{4,0},{8,12},{12,8},{16,20},{20,16},{24,28},{28,24},{1,5},{5... | collective-permute-start | bytes 1572872 | tf_op jit(solution)/shard_map/ppermute | solution.py:200
  68.9 17.4 %collective-permute-start.9 = (bf16[2048,128]{1,0:T(8,128)(2,1)S(1)}, bf16[2048,128]{1,0:T(8,128)(2,1)S(1)}, u32[]{:S(2)}, u32[]{:S(2)}) collective-permute-start(bf16[2048,128]{1,0:T(8,128)(2,1)S(1)} %bitcast.68), channel_id=1, source_target_pairs={{0,1},{3,2},{4,5},{7,6},{8,9},{11,10},{12,13},{15,14},{16,17},{19,... | collective-permute-start | bytes 1572872 | tf_op jit(solution)/shard_map/ppermute | solution.py:284
  82.3 13.4 %collective-permute-start.20 = (bf16[2048,128]{1,0:T(8,128)(2,1)S(1)}, bf16[2048,128]{1,0:T(8,128)(2,1)S(1)}, u32[]{:S(2)}, u32[]{:S(2)}) collective-permute-start(bf16[2048,128]{1,0:T(8,128)(2,1)S(1)} %bitcast.69), channel_id=1, source_target_pairs={{0,1},{3,2},{4,5},{7,6},{8,9},{11,10},{12,13},{15,14},{16,17},{19,... | collective-permute-start | bytes 1572872 | tf_op jit(solution)/shard_map/ppermute | solution.py:284
  83.6 22.1 %collective-permute-start.7 = (bf16[2048,128]{1,0:T(8,128)(2,1)S(1)}, bf16[2048,128]{1,0:T(8,128)(2,1)S(1)}, u32[]{:S(2)}, u32[]{:S(2)}) collective-permute-start(bf16[2048,128]{1,0:T(8,128)(2,1)S(1)} %bitcast.66), channel_id=1, source_target_pairs={{0,1},{1,2},{2,3},{4,5},{5,6},{6,7},{8,9},{9,10},{10,11},{12,13},{... | collective-permute-start | bytes 1572872 | tf_op jit(solution)/shard_map/ppermute | solution.py:284
  84.9 20.7 %collective-permute-start.8 = (bf16[2048,128]{1,0:T(8,128)(2,1)S(1)}, bf16[2048,128]{1,0:T(8,128)(2,1)S(1)}, u32[]{:S(2)}, u32[]{:S(2)}) collective-permute-start(bf16[2048,128]{1,0:T(8,128)(2,1)S(1)} %bitcast.64), channel_id=1, source_target_pairs={{1,0},{2,1},{3,2},{5,4},{6,5},{7,6},{9,8},{10,9},{11,10},{13,12},{... | collective-permute-start | bytes 1572872 | tf_op jit(solution)/shard_map/ppermute | solution.py:284
  86.3 43.6 %collective-permute-start.10 = (bf16[2048,128]{1,0:T(8,128)(2,1)S(1)}, bf16[2048,128]{1,0:T(8,128)(2,1)S(1)}, u32[]{:S(2)}, u32[]{:S(2)}) collective-permute-start(bf16[2048,128]{1,0:T(8,128)(2,1)S(1)} %fusion.8), channel_id=1, source_target_pairs={{0,2},{1,3},{3,1},{2,0},{4,6},{5,7},{7,5},{6,4},{8,10},{9,11},{11,... | collective-permute-start | bytes 1572872 | tf_op jit(solution)/shard_map/ppermute | solution.py:284
  91.7 38.9 %collective-permute-start.18 = (bf16[2048,128]{1,0:T(8,128)(2,1)S(1)}, bf16[2048,128]{1,0:T(8,128)(2,1)S(1)}, u32[]{:S(2)}, u32[]{:S(2)}) collective-permute-start(bf16[2048,128]{1,0:T(8,128)(2,1)S(1)} %bitcast.67), channel_id=1, source_target_pairs={{0,1},{1,2},{2,3},{4,5},{5,6},{6,7},{8,9},{9,10},{10,11},{12,13},{... | collective-permute-start | bytes 1572872 | tf_op jit(solution)/shard_map/ppermute | solution.py:284
  95.7 35.0 %collective-permute-start.19 = (bf16[2048,128]{1,0:T(8,128)(2,1)S(1)}, bf16[2048,128]{1,0:T(8,128)(2,1)S(1)}, u32[]{:S(2)}, u32[]{:S(2)}) collective-permute-start(bf16[2048,128]{1,0:T(8,128)(2,1)S(1)} %bitcast.65), channel_id=1, source_target_pairs={{1,0},{2,1},{3,2},{5,4},{6,5},{7,6},{9,8},{10,9},{11,10},{13,12},{... | collective-permute-start | bytes 1572872 | tf_op jit(solution)/shard_map/ppermute | solution.py:284
  97.0 33.2 %copy-start = (bf16[256,256]{1,0:T(8,128)(2,1)S(1)}, bf16[256,256]{1,0:T(8,128)(2,1)}, u32[]{:S(2)}) copy-start(bf16[256,256]{1,0:T(8,128)(2,1)} %param.12) | copy-start | bytes 393220
  97.0 33.2 %copy-start.1 = (f32[256]{0:T(256)S(1)}, f32[256]{0:T(256)}, u32[]{:S(2)}) copy-start(f32[256]{0:T(256)} %param.13) | copy-start | bytes 3076
  105.7 53.0 %collective-permute-start.21 = (bf16[2048,128]{1,0:T(8,128)(2,1)S(1)}, bf16[2048,128]{1,0:T(8,128)(2,1)S(1)}, u32[]{:S(2)}, u32[]{:S(2)}) collective-permute-start(bf16[2048,128]{1,0:T(8,128)(2,1)S(1)} %fusion.4), channel_id=1, source_target_pairs={{0,2},{1,3},{3,1},{2,0},{4,6},{5,7},{7,5},{6,4},{8,10},{9,11},{11,... | collective-permute-start | bytes 1572872 | tf_op jit(solution)/shard_map/ppermute | solution.py:284
